TPU v7x, 256 devices: a whole 4x4x8 slice. The times are simulated.
256 devices in a mesh: grp: 8 (over y_hi, x), dev: 32 (over z, y_lo, core).
Axes of the slice: x: 4, y: 4 (y_hi: 2, y_lo: 2; y = y_hi * 2 + y_lo), z: 8, core: 2. Of those that a mesh axis runs over, the one named last changes fastest.
Arguments:
- queries: bfloat16 [32768, 256], P(('grp', 'dev')), may hold values from -32 to 32
- items: bfloat16 [32768, 256], P(('grp', 'dev')), may hold values from -24 to 24
- item_ids: int32 [32768], P('grp'), may hold values from 0 to 262143
- neg_embed: bfloat16 [16384, 256], P('dev'), may hold values from -6 to 6
- neg_logq: float32 [16384], P('dev'), may hold values from -12 to -8
- logq_table: float32 [262144], replicated, may hold values from -11 to -9.5
Outputs:
- query_loss: float32 [32768], P(('grp', 'dev'))
- query_grad: float32 [32768, 256], P(('grp', 'dev'))
- item_grad: float32 [32768, 256], P(('grp', 'dev'))
- negative_grad: float32 [16384, 256], P('dev')
Inputs may be any that keep to these rules, and one draw needn't show every extreme that they name: `item_ids`: a row of logq_table.
All inputs are finite; a program needn't handle non-finite values.
Results may differ from a plain program's by a relative error of at most 0.0036.
Values may be sent and summed in bfloat16 or wider, within the bound.
A program may use at most 64 MiB of HBM per device.

v0:
```python
import jax
import jax.numpy as jnp
from jax import lax
from jax.sharding import PartitionSpec as P

logit_scale = 0.25


def from_everyone(shard, axis):
    length = lax.axis_size(axis)
    return lax.all_to_all(
        jnp.broadcast_to(shard[None], (length, *shard.shape)), axis, 0, 0, tiled=True
    )


def all_in_one(shard, axis):
    leaves = jax.tree.leaves(shard)
    order = sorted(range(len(leaves)), key=lambda k: -leaves[k].size)
    width = (1, *leaves[order[0]].shape)[-1]
    lines = [
        jnp.pad(leaves[k].reshape(-1), (0, -leaves[k].size % width)).reshape(-1, width)
        for k in order
    ]
    both, at, found = (from_everyone(jnp.concatenate(lines), axis), 0, {})
    for k, line in zip(order, lines):
        section = both[:, at : at + len(line)].reshape(len(both), -1)
        found[k] = section[:, : leaves[k].size].reshape(-1, *leaves[k].shape)
        at += len(line)
    numbers = iter(range(len(leaves)))
    return jax.tree.map(lambda _: found[next(numbers)], shard)


def folded_in_pairs(pieces, combine):
    while len(jax.tree.leaves(pieces)[0]) > 1:
        pieces = jax.vmap(combine)(
            *(jax.tree.map(lambda part: part[side::2], pieces) for side in (0, 1))
        )
    return jax.tree.map(lambda part: part[0], pieces)


def joined_all(shard, axis, combine):
    pieces = all_in_one(shard, axis)
    return folded_in_pairs(pieces, combine)


def cut_along(shard, dim, length):
    before, after = (shard.shape[:dim], shard.shape[dim + 1 :])
    return jnp.moveaxis(shard.reshape(*before, length, -1, *after), dim, 0)


def summed_on_arrival(shard, axis, dim):
    pieces = cut_along(shard, dim, lax.axis_size(axis))
    arrived = lax.all_to_all(pieces, axis, split_axis=0, concat_axis=0, tiled=True)
    return arrived.astype(jnp.float32).sum(axis=0)


def taken_together(shard, axis):
    return from_everyone(shard, axis).sum(axis=0)


def block_shape(all_rows):
    block_rows = min(512, all_rows)
    return (block_rows, all_rows // block_rows)


def combine_stats(earlier, later):
    row_max = jnp.maximum(earlier[0], later[0])
    return (
        row_max,
        earlier[1] * jnp.exp(earlier[0] - row_max) + later[1] * jnp.exp(later[0] - row_max),
    )


def log_total(maxima, totals):
    row_max, row_sum = joined_all((maxima, totals), "dev", combine_stats)
    return row_max + jnp.log(row_sum)


def row_stats(scores):
    row_max = jnp.max(scores, axis=1)
    return (row_max, jnp.sum(jnp.exp(scores - row_max[:, None]), axis=1))


def logits(q_block, candidates, cand_offsets):
    return (
        logit_scale * jnp.dot(q_block, candidates.T, preferred_element_type=jnp.float32)
        - cand_offsets[None, :]
    )


def local(queries, items, item_ids, neg_embed, neg_logq, logq_table):
    own_rows, feat_width = queries.shape
    dev_index = lax.axis_index("dev")
    own_start = dev_index * own_rows
    own_ids = lax.dynamic_slice_in_dim(item_ids, own_start, own_rows, 0)
    own_offsets = jnp.take(logq_table, own_ids, axis=0)
    group_q = lax.all_gather(queries, "dev", axis=0, tiled=True)
    all_rows = group_q.shape[0]
    block_rows, block_count = block_shape(all_rows)
    blocks = group_q.reshape(block_count, block_rows, feat_width)
    starts = jnp.arange(block_count, dtype=jnp.int32) * block_rows
    candidates = jnp.concatenate([items, neg_embed], axis=0)
    cand_offsets = jnp.concatenate([own_offsets, neg_logq], axis=0)
    columns = jnp.arange(candidates.shape[0], dtype=jnp.int32)

    def positives(first_row):
        targets = first_row + jnp.arange(block_rows, dtype=jnp.int32) - own_start
        return (columns[None, :] == targets[:, None]) & (columns[None, :] < own_rows)

    def forward(packed):
        q_block, first_row = packed
        scores = logits(q_block, candidates, cand_offsets)
        row_max, row_sum = row_stats(scores)
        return (row_max, row_sum, jnp.sum(jnp.where(positives(first_row), scores, 0.0), axis=1))

    maxima, totals, matched = lax.map(forward, (blocks, starts))
    log_norm = log_total(maxima.reshape(all_rows), totals.reshape(all_rows))
    own_norm = lax.dynamic_slice_in_dim(log_norm, own_start, own_rows, 0)
    own_match = lax.dynamic_slice_in_dim(matched.reshape(all_rows), own_start, own_rows, 0)
    query_loss = own_norm - own_match

    def backward(summed, packed):
        q_block, first_row, block_norm = packed
        scores = logits(q_block, candidates, cand_offsets)
        logit_grad = (
            logit_scale
            * (jnp.exp(scores - block_norm[:, None]) - positives(first_row).astype(jnp.float32))
        ).astype(jnp.bfloat16)
        summed = summed + jnp.einsum(
            "rc,rd->cd", logit_grad, q_block, preferred_element_type=jnp.float32
        )
        return (summed, jnp.dot(logit_grad, candidates, preferred_element_type=jnp.float32))

    zero_acc = jnp.zeros((candidates.shape[0], feat_width), jnp.float32)
    cand_grad, q_partial = lax.scan(
        backward, zero_acc, (blocks, starts, log_norm.reshape(block_count, block_rows))
    )
    query_grad = summed_on_arrival(
        q_partial.reshape(all_rows, feat_width).astype(jnp.bfloat16), "dev", 0
    )
    item_grad = cand_grad[:own_rows]
    negative_part = cand_grad[own_rows:]
    negative_grad = taken_together(negative_part, "grp")
    return (query_loss, query_grad, item_grad, negative_grad)


def solution(mesh):
    return jax.shard_map(
        local,
        mesh=mesh,
        in_specs=(
            P(("grp", "dev"), None),
            P(("grp", "dev"), None),
            P("grp"),
            P("dev", None),
            P("dev"),
            P(),
        ),
        out_specs=(
            P(("grp", "dev")),
            P(("grp", "dev"), None),
            P(("grp", "dev"), None),
            P("dev", None),
        ),
        check_vma=False,
    )
```

profile of v0, /device:TPU:1, one launch (start us, length us, event | category | flops | bytes accessed | tf_op | source)
XLA Modules:
  0.0 316.2 jit_solution(15767919707973878997)
XLA Ops:
  13.2 65.3 %all-gather.2.cloned.1.call-done = bf16[4096,256]{1,0:T(8,128)(2,1)} async-done(((bf16[128,256]{1,0:T(8,128)(2,1)}), bf16[4096,256]{1,0:T(8,128)(2,1)}) %all-gather.2.cloned.1.call-update) | async-done | bytes 2097168 | tf_op jit(solution)/shard_map/all_gather | solution.py:97
  78.5 28.9 %while.30 = (s32[]{:T(128)}, f32[8,512]{1,0:T(8,128)S(1)}, f32[8,512]{1,0:T(8,128)S(1)}, f32[8,512]{1,0:T(8,128)S(1)}, bf16[8,512,256]{2,1,0:T(8,128)(2,1)}, /*i...) while((s32[]{:T(128)}, f32[8,512]{1,0:T(8,128)S(1)}, ...), condition=%wide.region_4.5_spmd.clone.clone, body=%wide.region_0.4_spmd.clone.clone.sunk | while | flops 170721408 | bytes 3239833 | solution.py:116
  90.5 1.4 fusion.44
  94.2 1.4 fusion.44
  97.8 1.4 fusion.44
  101.4 1.4 fusion.44
  105.0 1.4 fusion.44
  107.5 1.5 broadcast_in_dim.56
  108.9 6.6 %all-to-all-start = ((f32[32,2,4096]{2,1,0:T(2,128)}), f32[32,2,4096]{2,1,0:T(2,128)S(1)}, u32[]{:S(2)}, u32[]{:S(2)}) async-start(f32[32,2,4096]{2,1,0:T(2,128)} %broadcast_in_dim.56), calls=%async_computation | async-start | bytes 2097152 | tf_op jit(solution)/shard_map/all_to_all | solution.py:11
  115.5 28.1 %all-to-all-done = f32[32,2,4096]{2,1,0:T(2,128)S(1)} async-done(((f32[32,2,4096]{2,1,0:T(2,128)}), f32[32,2,4096]{2,1,0:T(2,128)S(1)}, u32[]{:S(2)}, u32[]{:S(2)}) %all-to-all-start) | async-done | bytes 1048608 | tf_op jit(solution)/shard_map/all_to_all | solution.py:11
  150.5 43.4 %while.31 = (s32[]{:T(128)}, f32[640,256]{1,0:T(8,128)S(1)}, bf16[8,512,256]{2,1,0:T(8,128)(2,1)}, bf16[8,512,256]{2,1,0:T(8,128)(2,1)}, bf16[640,256]{1,0:T(8,1...) while((s32[]{:T(128)}, f32[640,256]{1,0:T(8,128)S(1)}, ...), condition=%wide.region_6.7_spmd.clone.clone, body=%wide.region_5.6_spmd.clone.clone.sunk | while | flops 506594944 | bytes 4994979 | solution.py:135
  151.8 1.6 fusion.51
  153.4 1.5 convolution_add_fusion.2
  157.2 1.6 fusion.51
  158.8 1.5 convolution_add_fusion.2
  162.6 1.6 fusion.51
  164.2 1.5 convolution_add_fusion.2
  168.1 1.6 fusion.51
  169.6 1.5 convolution_add_fusion.2
  173.5 1.6 fusion.51
  175.1 1.5 convolution_add_fusion.2
  178.9 1.6 fusion.51
  180.5 1.5 convolution_add_fusion.2
  184.3 1.6 fusion.51
  185.9 1.5 convolution_add_fusion.2
  189.7 1.6 fusion.51
  191.3 1.5 convolution_add_fusion.2
  194.3 56.0 %all_to_all.15 = f32[8,512,256]{2,1,0:T(8,128)} all-to-all(f32[8,512,256]{2,1,0:T(8,128)S(1)} %broadcast_in_dim.59), channel_id=1, replica_groups=mesh['grp'=8,'dev'=32] {'grp'}, dimensions={0} | all-to-all | bytes 8388608 | tf_op jit(solution)/shard_map/all_to_all | solution.py:11
  250.3 6.4 %all-to-all-start.1 = ((bf16[32,128,256]{2,1,0:T(8,128)(2,1)}), bf16[32,128,256]{2,1,0:T(8,128)(2,1)}, u32[]{:S(2)}, u32[]{:S(2)}) async-start(bf16[32,128,256]{2,1,0:T(8,128)(2,1)} %bitcast.72), calls=%async_computation.1 | async-start | bytes 4194304 | tf_op jit(solution)/shard_map/all_to_all | solution.py:53
  258.0 3.3 %reduce_sum.37 = f32[512,256]{1,0:T(8,128)} reduce(f32[8,512,256]{2,1,0:T(8,128)} %all_to_all.15, f32[]{:T(128)} %constant.43.clone.1), dimensions={0}, to_apply=%region_8.9 | reduce | flops 917504 | bytes 4718596 | tf_op jit(solution)/shard_map/reduce_sum | solution.py:58
  261.3 45.5 %all-to-all-done.1 = bf16[32,128,256]{2,1,0:T(8,128)(2,1)} async-done(((bf16[32,128,256]{2,1,0:T(8,128)(2,1)}), bf16[32,128,256]{2,1,0:T(8,128)(2,1)}, u32[]{:S(2)}, u32[]{:S(2)}) %all-to-all-start.1) | async-done | bytes 2097184 | tf_op jit(solution)/shard_map/all_to_all | solution.py:53
  306.8 2.5 convert_reduce_fusion
  (149 shorter events, 54.3 us)
Async XLA Ops:
  7.2 1.6 copy-start
  7.2 71.3 %all-gather.2.cloned.1.call-start = ((), (), s32[]{:S(2)}) async-start(), calls=%async_computation.3 | async-start | bytes 2162688 | tf_op jit(solution)/shard_map/all_gather | solution.py:97
  108.9 34.7 %all-to-all-start = ((f32[32,2,4096]{2,1,0:T(2,128)}), f32[32,2,4096]{2,1,0:T(2,128)S(1)}, u32[]{:S(2)}, u32[]{:S(2)}) async-start(f32[32,2,4096]{2,1,0:T(2,128)} %broadcast_in_dim.56), calls=%async_computation | async-start | bytes 2097152 | tf_op jit(solution)/shard_map/all_to_all | solution.py:11
  250.3 56.5 %all-to-all-start.1 = ((bf16[32,128,256]{2,1,0:T(8,128)(2,1)}), bf16[32,128,256]{2,1,0:T(8,128)(2,1)}, u32[]{:S(2)}, u32[]{:S(2)}) async-start(bf16[32,128,256]{2,1,0:T(8,128)(2,1)} %bitcast.72), calls=%async_computation.1 | async-start | bytes 4194304 | tf_op jit(solution)/shard_map/all_to_all | solution.py:53
Sparse Core Ops, SparseCore 0:
  9.8 68.5 all-gather.1
where the time goes:
time: 318 us; the launch traced here: 316 us
  waiting for transfers between devices  140 us (44%)
  blocking collectives  56 us (18%)
  matrix products  44.7 us (14%)
  other arithmetic  26.7 us (8%)
  local copies, waits for them, and re-layouts  21.2 us (7%)
  between operations  14.3 us (4%)
  starting transfers between devices  13.1 us (4%)
    all_gather x1, waiting for transfers between devices, local(): group_q = lax.all_gather(queries, 'dev', axis=0, tiled=True)  65.3 us
    all_to_all x1, blocking collectives, from_everyone(): lax.all_to_all(jnp.broadcast_to(shard[None], (length, *shard.shape)), axi...  56 us
    all_to_all x1, waiting for transfers between devices, summed_on_arrival(): lax.all_to_all(pieces, axis, split_axis=0, concat_axis=0, tiled=True)  45.5 us
    all_to_all x1, waiting for transfers between devices, from_everyone(): lax.all_to_all(jnp.broadcast_to(shard[None], (length, *shard.shape)), axi...  28.1 us
    dot_general x16, matrix products, logits(): jnp.dot(q_block, candidates.T, preferred_element_type=jnp.float32)  24.2 us
    dot_general x8, matrix products, backward(): jnp.einsum('rc,rd->cd', logit_grad, q_block, preferred_element_type=jnp.f...  11.8 us
    sub x16, other arithmetic, positives(): targets = first_row + jnp.arange(block_rows, dtype=jnp.int32) - own_start  10.4 us
    dynamic_slice x16, local copies, waits for them, and re-layouts, local(): maxima, totals, matched = lax.map(forward, (blocks, starts))  9.35 us
  transfers between devices with their start and end apart: 3, of which 3 were waited for; matrix products, arithmetic and copies ran while one was open for 3% of the time, Pallas kernels for 0%

commit v1 on v0

v1 whole, which is shorter than its diff:
```python
import functools

import jax
import jax.numpy as jnp
from jax import lax
from jax.experimental import pallas as pl
from jax.experimental.pallas import tpu as pltpu
from jax.sharding import PartitionSpec as P

MESH = pl.DeviceIdType.MESH
SCALE = 0.25
MASKED = -1e30
LANES = 128


def pair_order(nz):
    order = []
    for r in range(1, nz // 2):
        order += [r, nz - r]
    return order + [0, nz // 2]


def kernel(
    nz,
    nx,
    q_ref,
    v_ref,
    ids_ref,
    neg_ref,
    nlq_ref,
    tab_ref,
    loss_ref,
    qg_ref,
    vg_ref,
    ng_ref,
    q_all,
    cand,
    cand_t,
    offs,
    off_b,
    gat,
    scores,
    probs,
    probs2,
    cgrad,
    part,
    part_in,
    stat,
    stat_in,
    lz,
    lz_in,
    d2d_in,
    itm,
    itm_in,
    rs,
    rs_in,
    red,
    ag,
    q_sem,
    item_sem,
    neg_sem,
    off_sem,
    stat_sem,
    lz_sem,
    part_sem,
    d2d_sem,
    itm_sem,
    rs_sem,
    ag_sem,
):
    rows, width = q_ref.shape
    neg_rows = neg_ref.shape[0]
    shard = rows + neg_rows
    nyh = 2
    groups = nyh * nx
    cut = neg_rows // groups
    order = pair_order(nz)
    pos = {r: i for i, r in enumerate(order)}
    pairs = nz // 2

    g = lax.axis_index("grp")
    d = lax.axis_index("dev")
    yh, x = g // nx, g % nx
    z, yl, c = d // 4, (d // 2) % 2, d % 2

    def at(zz, dyl, dc):
        return zz * 4 + ((yl + dyl) % 2) * 2 + (c + dc) % 2

    def grp_at(dyh, dx):
        return ((yh + dyh) % 2) * nx + (x + dx) % nx

    def z_dev(r):
        return (g, at((z + r) % nz, 0, 0))

    plane = [
        (dyh, dx, dyl) for dyl in range(2) for dyh in range(nyh) for dx in range(nx)
    ]

    def mirror(dyh, dx, dyl):
        return plane.index((dyh, (nx - dx) % nx, dyl))

    started = []

    def push(src, dst, sems, i, device):
        copy = pltpu.make_async_remote_copy(
            src_ref=src,
            dst_ref=dst,
            send_sem=sems.at[0, i],
            recv_sem=sems.at[1, i],
            device_id=device,
            device_id_type=MESH,
        )
        copy.start()
        started.append(copy)
        return copy

    peers = [z_dev(r) for r in range(1, nz)]
    peers += [(g, at(z, j // 2, j % 2)) for j in (1, 2, 3)]
    peers += [(grp_at(1, 0), at(z, 1, 1))]
    peers += [
        (grp_at(dyh, dx), at(z, dyl, 0))
        for dyh, dx, dyl in plane
        if (dyh, dx) != (0, 0)
    ]
    barrier = pltpu.get_barrier_semaphore()
    for peer in peers:
        pl.semaphore_signal(barrier, inc=1, device_id=peer, device_id_type=MESH)

    def look(i, carry):
        entry = ids_ref[d * rows + i]
        row = tab_ref[pl.ds(lax.shift_right_logical(entry, 7), 1), :]
        lane = lax.broadcasted_iota(jnp.int32, (1, LANES), 1)
        gat[pl.ds(i, 1), :] = jnp.where(lane == (entry & 127), row, 0.0)
        return carry

    lax.fori_loop(0, rows, look, 0, unroll=8)
    offs[0, 0:1, :] = jnp.sum(gat[...].T, axis=0, keepdims=True)
    offs[0, 1 : 1 + neg_rows // LANES, :] = nlq_ref[...]

    pl.semaphore_wait(barrier, len(peers))

    q_copies, item_copies, neg_copies, off_copies = {}, {}, {}, {}
    for j in (1, 2, 3):
        device = (g, at(z, j // 2, j % 2))
        off_copies[j] = push(offs.at[0], offs.at[j], off_sem, j, device)
    for r in order:
        if r:
            q_copies[r] = push(
                q_ref, q_all.at[pl.ds(pos[r] * rows, rows)], q_sem, r, z_dev(nz - r)
            )
    for j in (1, 2, 3):
        device = (g, at(z, j // 2, j % 2))
        neg_device = (grp_at(1, 0), at(z, 1, 1)) if j == 3 else device
        item_copies[j] = push(
            v_ref, cand.at[pl.ds(j * shard, rows)], item_sem, j, device
        )
        neg_copies[j] = push(
            neg_ref, cand.at[pl.ds(j * shard + rows, neg_rows)], neg_sem, j, neg_device
        )

    q_all[pos[0] * rows : (pos[0] + 1) * rows, :] = q_ref[...]
    cand[0:rows, :] = v_ref[...]
    cand[rows:shard, :] = neg_ref[...]

    for j in range(4):
        if j:
            off_copies[j].wait_recv()
            item_copies[j].wait_recv()
            neg_copies[j].wait_recv()

        def turn(k, carry, j=j):
            line = jnp.broadcast_to(offs[j, pl.ds(k, 1), :], (LANES, LANES))
            off_b[pl.ds(j * shard + k * LANES, LANES), :] = line.T
            return carry

        lax.fori_loop(0, shard // LANES, turn, 0)
        for k in range(shard // LANES):
            lo = j * shard + k * LANES
            cand_t[:, lo : lo + LANES] = cand[lo : lo + LANES, :].T

    eye = lax.broadcasted_iota(jnp.int32, (rows, rows), 0) == lax.broadcasted_iota(
        jnp.int32, (rows, rows), 1
    )
    own_score = None
    tall = 4 * shard
    maxima = [None] * pairs

    def dot_nt(a, b):
        return lax.dot_general(
            a, b, (((1,), (1,)), ((), ())), preferred_element_type=jnp.float32
        )

    def fold(s, op):
        return op(s.reshape(s.shape[0] // 8, 8, s.shape[1]), axis=0)

    stat_copies = {}
    for p in range(pairs):
        for r in order[2 * p : 2 * p + 2]:
            if r:
                q_copies[r].wait_recv()
        scaled = q_all[2 * p * rows : (2 * p + 2) * rows, :] * jnp.bfloat16(SCALE)

        def slot_scores(j, scaled=scaled):
            s = dot_nt(cand[pl.ds(j * shard, shard), :], scaled)
            ob = off_b[pl.ds(j * shard, shard), :]
            return s - jnp.concatenate([ob, ob], axis=1)

        def forward(j, top, p=p, slot_scores=slot_scores):
            s = slot_scores(j)
            scores[p, pl.ds(j * shard, shard), :] = s
            return jnp.maximum(top, fold(s, jnp.max))

        if p == pairs - 1:
            s = slot_scores(0)
            corner = s[:rows, :rows]
            own_score = jnp.sum(jnp.where(eye, corner, 0.0), axis=0, keepdims=True)
            corner = jnp.where(eye, MASKED, corner)
            s = jnp.concatenate(
                [jnp.concatenate([corner, s[:rows, rows:]], axis=1), s[rows:]], axis=0
            )
            scores[p, 0:shard, :] = s
            top, first = fold(s, jnp.max), 1
        else:
            top, first = jnp.full((8, 2 * rows), MASKED, jnp.float32), 0
        top = lax.fori_loop(first, 4, forward, top)
        top = jnp.max(top, axis=0, keepdims=True)

        def weigh(t, total, p=p, top=top):
            e = jnp.exp(scores[p, pl.ds(t * LANES, LANES), :] - top)
            probs[pl.ds(t * LANES, LANES), :] = e.astype(jnp.bfloat16)
            return total + fold(e, jnp.sum)

        total = lax.fori_loop(
            0, tall // LANES, weigh, jnp.zeros((8, 2 * rows), jnp.float32)
        )
        total = jnp.sum(total, axis=0, keepdims=True)
        for h in range(2):
            r = order[2 * p + h]
            lanes = slice(h * rows, (h + 1) * rows)
            both = jnp.concatenate(
                [top[:, lanes], total[:, lanes], jnp.zeros((6, rows), jnp.float32)], axis=0
            )
            if r:
                stat[2 * p + h] = both
                back = nz - r
                stat_copies[back] = push(
                    stat.at[2 * p + h], stat_in.at[back], stat_sem, back, z_dev(r)
                )
            else:
                stat_in[0] = both
        qp = jnp.dot(cand_t[...], probs[...], preferred_element_type=jnp.float32)
        for h in range(2):
            part[2 * p + h] = qp[:, h * rows : (h + 1) * rows].astype(jnp.bfloat16)

    for r in range(1, nz):
        stat_copies[r].wait_recv()
    best = own_score
    for r in range(nz):
        best = jnp.maximum(best, stat_in[r, 0:1, :])
    mass = jnp.exp(own_score - best)
    for r in range(nz):
        mass = mass + stat_in[r, 1:2, :] * jnp.exp(stat_in[r, 0:1, :] - best)
    log_norm = best + jnp.log(mass)
    lz[...] = jnp.broadcast_to(log_norm, (8, rows))
    lz_copies = {}
    for r in order:
        if r:
            lz_copies[r] = push(lz, lz_in.at[pos[r]], lz_sem, r, z_dev(nz - r))
    lz_in[pos[0]] = jnp.broadcast_to(log_norm, (8, rows))
    loss_ref[...] = log_norm - own_score
    own_term = jnp.exp(own_score - log_norm) - 1.0

    part_copies = {}
    for r in order:
        if r:
            back = nz - r
            part_copies[back] = push(
                part.at[pos[r]], part_in.at[back], part_sem, back, z_dev(r)
            )

    for r in order:
        if r:
            lz_copies[r].wait_recv()

    d2d_copies = []
    core_mate = (g, at(z, 0, 1))
    for j in (1, 3, 0, 2):

        def again(t, carry, j=j):
            lo = j * shard + t * 64
            for p in range(pairs):
                norm = jnp.concatenate(
                    [lz_in[2 * p, 0:1, :], lz_in[2 * p + 1, 0:1, :]], axis=1
                )
                e = jnp.exp(scores[p, pl.ds(lo, 64), :] - norm)
                probs2[pl.ds(t * 64, 64), 2 * p * rows : (2 * p + 2) * rows] = e.astype(
                    jnp.bfloat16
                )
            return carry

        lax.fori_loop(0, shard // 64, again, 0)
        cgrad[j] = SCALE * jnp.dot(
            probs2[...], q_all[...], preferred_element_type=jnp.float32
        )
        if j in (1, 3):
            i = j // 2
            d2d_copies.append(push(cgrad.at[j], d2d_in.at[i], d2d_sem, i, core_mate))

    for i in range(2):
        d2d_copies[i].wait_recv()
    itm[...] = (cgrad[2, 0:rows, :] + d2d_in[1, 0:rows, :]).astype(jnp.bfloat16)
    rs_copies = {}
    for dyl in (1, 0):
        j = 2 * dyl
        rs[dyl] = (cgrad[j, rows:shard, :] + d2d_in[dyl, rows:shard, :]).astype(jnp.bfloat16)
        for dyh, dx, dy in plane:
            if dy == dyl and (dyh, dx, dy) != (0, 0, 0):
                target = grp_at(dyh, dx)
                i = mirror(dyh, dx, dy)
                rs_copies[i] = push(
                    rs.at[dyl, pl.ds(pl.multiple_of(target * cut, cut), cut)],
                    rs_in.at[i],
                    rs_sem,
                    i,
                    (target, at(z, dyl, 0)),
                )
    itm_copy = push(itm, itm_in, itm_sem, 0, (g, at(z, 1, 0)))

    own_rows = pl.ds(pl.multiple_of(g * cut, cut), cut)
    own_neg = pl.ds(pl.multiple_of(rows + g * cut, cut), cut)
    summed = cgrad[0, own_neg, :] + d2d_in[0, own_neg, :]
    for i in range(1, len(plane)):
        rs_copies[i].wait_recv()
        summed = summed + rs_in[i].astype(jnp.float32)
    red[...] = summed.astype(jnp.bfloat16)
    ag_copies = {}
    for dyh, dx, dyl in plane:
        if dyl == 0 and (dyh, dx) != (0, 0):
            i = mirror(dyh, dx, 0)
            ag_copies[i] = push(
                red, ag.at[own_rows], ag_sem, i, (grp_at(dyh, dx), at(z, 0, 0))
            )
    ag[own_rows, :] = summed.astype(jnp.bfloat16)

    acc = own_term * cand_t[:, 0:rows].astype(jnp.float32)
    for r in range(nz):
        if r:
            part_copies[r].wait_recv()
            piece = part_in[r]
        else:
            piece = part[pos[0]]
        share = jnp.exp(stat_in[r, 0:1, :] - log_norm)
        acc = acc + share * piece.astype(jnp.float32)
    qg_ref[...] = (SCALE * acc).T

    itm_copy.wait_recv()
    column = jnp.broadcast_to(own_term, (rows, rows)).T
    column = jnp.concatenate([column] * (width // rows), axis=1)
    vg_ref[...] = (
        cgrad[0, 0:rows, :]
        + d2d_in[0, 0:rows, :]
        + itm_in[...].astype(jnp.float32)
        + SCALE * column * q_ref[...].astype(jnp.float32)
    )

    for i in ag_copies:
        ag_copies[i].wait_recv()
    ng_ref[...] = ag[...].astype(jnp.float32)
    for copy in started:
        copy.wait_send()


def local(queries, items, item_ids, neg_embed, neg_logq, logq_table, *, nz, nx):
    rows, width = queries.shape
    neg_rows = neg_embed.shape[0]
    shard = rows + neg_rows
    tall = 4 * shard
    groups = 2 * nx
    cut = neg_rows // groups
    f32, bf16 = jnp.float32, jnp.bfloat16
    dma = pltpu.SemaphoreType.DMA
    vmem = pl.BlockSpec(memory_space=pltpu.VMEM)
    smem = pl.BlockSpec(memory_space=pltpu.SMEM)
    loss, qg, vg, ng = pl.pallas_call(
        functools.partial(kernel, nz, nx),
        out_shape=(
            jax.ShapeDtypeStruct((1, rows), f32),
            jax.ShapeDtypeStruct((rows, width), f32),
            jax.ShapeDtypeStruct((rows, width), f32),
            jax.ShapeDtypeStruct((neg_rows, width), f32),
        ),
        in_specs=[vmem, vmem, smem, vmem, vmem, vmem],
        out_specs=(vmem, vmem, vmem, vmem),
        scratch_shapes=[
            pltpu.VMEM((nz * rows, width), bf16),
            pltpu.VMEM((tall, width), bf16),
            pltpu.VMEM((width, tall), bf16),
            pltpu.VMEM((4, 8, LANES), f32),
            pltpu.VMEM((tall, LANES), f32),
            pltpu.VMEM((rows, LANES), f32),
            pltpu.VMEM((nz // 2, tall, 2 * rows), f32),
            pltpu.VMEM((tall, 2 * rows), bf16),
            pltpu.VMEM((shard, nz * rows), bf16),
            pltpu.VMEM((4, shard, width), f32),
            pltpu.VMEM((nz, width, rows), bf16),
            pltpu.VMEM((nz, width, rows), bf16),
            pltpu.VMEM((nz, 8, rows), f32),
            pltpu.VMEM((nz, 8, rows), f32),
            pltpu.VMEM((8, rows), f32),
            pltpu.VMEM((nz, 8, rows), f32),
            pltpu.VMEM((2, shard, width), f32),
            pltpu.VMEM((rows, width), bf16),
            pltpu.VMEM((rows, width), bf16),
            pltpu.VMEM((2, neg_rows, width), bf16),
            pltpu.VMEM((2 * groups, cut, width), bf16),
            pltpu.VMEM((cut, width), bf16),
            pltpu.VMEM((neg_rows, width), bf16),
            dma((2, nz)),
            dma((2, 4)),
            dma((2, 4)),
            dma((2, 4)),
            dma((2, nz)),
            dma((2, nz)),
            dma((2, nz)),
            dma((2, 2)),
            dma((2, 1)),
            dma((2, 2 * groups)),
            dma((2, 2 * groups)),
        ],
        compiler_params=pltpu.CompilerParams(
            collective_id=0, has_side_effects=True, vmem_limit_bytes=60 << 20
        ),
    )(
        queries,
        items,
        item_ids,
        neg_embed,
        neg_logq.reshape(-1, LANES),
        logq_table.reshape(-1, LANES),
    )
    return loss.reshape(rows), qg, vg, ng


def solution(mesh):
    return jax.shard_map(
        functools.partial(
            local, nz=mesh.shape["dev"] // 4, nx=mesh.shape["grp"] // 2
        ),
        mesh=mesh,
        in_specs=(
            P(("grp", "dev"), None),
            P(("grp", "dev"), None),
            P("grp"),
            P("dev", None),
            P("dev"),
            P(),
        ),
        out_specs=(
            P(("grp", "dev")),
            P(("grp", "dev"), None),
            P(("grp", "dev"), None),
            P("dev", None),
        ),
        check_vma=False,
    )
```

time: 318 us -> 67 us (0.21)
  waiting for transfers between devices: 140 us -> 0 us
  Pallas kernels: 0 us -> 60.6 us
  blocking collectives: 56 us -> 0 us
  matrix products: 44.7 us -> 0 us
  other arithmetic: 26.7 us -> 0 us
  local copies, waits for them, and re-layouts: 21.2 us -> 5.12 us
  between operations: 14.3 us -> 0.65 us
  starting transfers between devices: 13.1 us -> 0 us
    all_to_all x2 -> x0, waiting for transfers between devices: 73.6 us -> none  [the longest x1 45.5 us: summed_on_arrival(): lax.all_to_all(pieces, axis, split_axis=0, concat_axis=0, tiled=True)]
    all_gather x1 -> x0, waiting for transfers between devices: 65.3 us -> none  [local(): group_q = lax.all_gather(queries, 'dev', axis=0, tiled=True)]
    pallas_call x0 -> x1, Pallas kernels: none -> 60.6 us  [local(): pl.pallas_call(functools.partial(kernel, nz, nx), out_shape=(jax.ShapeDty...]
    all_to_all x1 -> x0, blocking collectives: 56 us -> none  [from_everyone(): lax.all_to_all(jnp.broadcast_to(shard[None], (length, *shard.shape)), axi...]
    dot_general x32 -> x0, matrix products: 44.7 us -> none  [the longest x16 24.2 us: logits(): jnp.dot(q_block, candidates.T, preferred_element_type=jnp.float32)]
    all_to_all x2 -> x0, starting transfers between devices: 13.1 us -> none  [the longest x1 6.61 us: from_everyone(): lax.all_to_all(jnp.broadcast_to(shard[None], (length, *shard.shape)), axi...]
    reduce_sum x10 -> x0, other arithmetic: 11.5 us -> none  [the longest x8 5.6 us: forward(): jnp.sum(jnp.where(positives(first_row), scores, 0.0), axis=1)]
    sub x17 -> x0, other arithmetic: 10.9 us -> none  [the longest x16 10.4 us: positives(): targets = first_row + jnp.arange(block_rows, dtype=jnp.int32) - own_start]
  transfers between devices with their start and end apart: 3 -> 0, of which waited for: 3 -> 0; matrix products, arithmetic and copies ran while one was open for 3% -> 0% of each run, Pallas kernels for 0% -> 0%
where the time goes in v1:
time: 67 us; the launch traced here: 66.4 us
  Pallas kernels  60.6 us (90%)
  local copies, waits for them, and re-layouts  5.12 us (8%)
    pallas_call x1, Pallas kernels, local(): pl.pallas_call(functools.partial(kernel, nz, nx), out_shape=(jax.ShapeDty...  60.6 us
    unnamed x6, local copies, waits for them, and re-layouts  5.12 us

profile of v1, /device:TPU:1, one launch (start us, length us, event | category | flops | bytes accessed | tf_op | source)
XLA Modules:
  0.0 66.4 jit_solution(6888555267796922535)
XLA Ops:
  0.6 60.6 %shard_map.93 = (f32[1,128]{1,0:T(1,128)}, f32[128,256]{1,0:T(8,128)}, f32[128,256]{1,0:T(8,128)}, f32[512,256]{1,0:T(8,128)}) custom-call(bf16[128,256]{1,0:T(8,128)(2,1)} %q_ref.1, bf16[128,256]{1,0:T(8,128)(2,1)} %v_ref.1, s32[4096]{0:T(1024)} %ids_ref.1, bf16[512,256]{1,0:T(8,128)(2,1)} %neg_ref.1, f32[4,128]{1,0:T(4,128)} %bitcast.4, f32[2048,128]{1,0:T(8,128)} %bitcast.3), custom_call_target="tpu_custom_call" | custom-call | tf_op jit(solution)/shard_map/pallas_call | solution.py:384
  61.3 0.0 copy-start
  61.3 1.2 %copy.14 = f32[128]{0:T(128)} copy(f32[128]{0:T(128)} %bitcast.5) | data formatting | bytes 1024
  62.5 1.6 %copy.15 = f32[128,256]{1,0:T(8,128)} copy(f32[128,256]{1,0:T(8,128)} %get-tuple-element.17) | data formatting | bytes 262144
  64.0 1.6 %copy.16 = f32[128,256]{1,0:T(8,128)} copy(f32[128,256]{1,0:T(8,128)} %get-tuple-element.18) | data formatting | bytes 262144
  65.6 0.0 copy-done
  65.6 0.8 %copy.17 = f32[512,256]{1,0:T(8,128)} copy(f32[512,256]{1,0:T(8,128)S(1)} %copy-done) | data formatting | bytes 1048576
Async XLA Ops:
  61.3 4.3 %copy-start = (f32[512,256]{1,0:T(8,128)S(1)}, f32[512,256]{1,0:T(8,128)}, u32[]{:S(2)}) copy-start(f32[512,256]{1,0:T(8,128)} %get-tuple-element.19) | copy-start | bytes 1572868

commit v2 on v1

v2 whole, which is shorter than its diff:
```python
import functools

import jax
import jax.numpy as jnp
from jax import lax
from jax.experimental import pallas as pl
from jax.experimental.pallas import tpu as pltpu
from jax.sharding import PartitionSpec as P

MESH = pl.DeviceIdType.MESH
SCALE = 0.25
MASKED = -1e30
LANES = 128
DIRECT = 192


def pair_order(nz):
    order = [0, 1]
    for r in range(1, nz // 2):
        order += [nz - r, r + 1]
    return order


def dot_nt(a, b):
    return lax.dot_general(
        a, b, (((1,), (1,)), ((), ())), preferred_element_type=jnp.float32
    )


def fold(s, op):
    return op(s.reshape(s.shape[0] // 8, 8, s.shape[1]), axis=0)


def kernel(
    nz,
    nx,
    q_hbm,
    v_hbm,
    ids_hbm,
    neg_hbm,
    nlq_hbm,
    tab_hbm,
    loss_ref,
    qg_ref,
    vg_ref,
    ag,
    ids_ref,
    tab_ref,
    nlq_ref,
    q_all,
    cand,
    cand_t,
    offs,
    off_b,
    gat,
    scores,
    probs,
    probs2,
    cgrad,
    part,
    part_in,
    stat,
    stat_in,
    lz,
    lz_in,
    d2d,
    d2d_in,
    itm,
    itm_in,
    rs,
    rs_in,
    red,
    in_sem,
    q_sem,
    cand_sem,
    off_sem,
    stat_sem,
    lz_sem,
    part_sem,
    d2d_sem,
    itm_sem,
    rs_sem,
    ag_sem,
):
    rows, width = qg_ref.shape
    neg_rows = ag.shape[0]
    shard = rows + neg_rows
    tall = 4 * shard
    nyh = 2
    groups = nyh * nx
    cut = neg_rows // groups
    order = pair_order(nz)
    pos = {r: i for i, r in enumerate(order)}
    pairs = nz // 2
    early = max(1, pairs // 2)
    ahead = max(0, pairs - 2)

    g = lax.axis_index("grp")
    d = lax.axis_index("dev")
    yh, x = g // nx, g % nx
    z, yl, c = d // 4, (d // 2) % 2, d % 2

    def at(zz, dyl, dc):
        return zz * 4 + ((yl + dyl) % 2) * 2 + (c + dc) % 2

    def grp_at(dyh, dx):
        return ((yh + dyh) % 2) * nx + (x + dx) % nx

    def z_dev(r):
        return (g, at((z + r) % nz, 0, r))

    def distance(dyh, dx, dyl):
        return min(dx, nx - dx) + (1 if dyl else 2 * dyh)

    plane = [
        (dyh, dx, dyl) for dyl in range(2) for dyh in range(nyh) for dx in range(nx)
    ]
    far_first = sorted(plane, key=lambda t: -distance(*t))

    def mirror(dyh, dx, dyl):
        return plane.index((dyh, (nx - dx) % nx, dyl))

    started = []

    def push(src, dst, sems, i, device):
        copy = pltpu.make_async_remote_copy(
            src_ref=src,
            dst_ref=dst,
            send_sem=sems.at[0, i],
            recv_sem=sems.at[1, i],
            device_id=device,
            device_id_type=MESH,
        )
        copy.start()
        started.append(copy)
        return copy

    def rows_of(start, size):
        return pl.ds(start, size)

    loads = [
        pltpu.make_async_copy(q_hbm, q_all.at[rows_of(0, rows)], in_sem.at[0]),
        pltpu.make_async_copy(v_hbm, cand.at[rows_of(0, rows)], in_sem.at[1]),
        pltpu.make_async_copy(neg_hbm, cand.at[rows_of(rows, neg_rows)], in_sem.at[2]),
        pltpu.make_async_copy(ids_hbm, ids_ref, in_sem.at[3]),
        pltpu.make_async_copy(tab_hbm, tab_ref, in_sem.at[4]),
        pltpu.make_async_copy(nlq_hbm, nlq_ref, in_sem.at[5]),
    ]
    for load in loads:
        load.start()

    core_mate = (g, at(z, 0, 1))
    y_mate = (g, at(z, 1, 0))
    y_wrap = (grp_at(1, 0), at(z, 1, 0))
    peers = [z_dev(r) for r in range(1, nz)]
    peers += [(g, at(z, j // 2, j % 2)) for j in (1, 2, 3)]
    peers += [y_wrap]
    peers += [
        (grp_at(dyh, dx), at(z, dyl, 1))
        for dyh, dx, dyl in plane
        if (dyh, dx) != (0, 0)
    ]
    barrier = pltpu.get_barrier_semaphore()
    for peer in peers:
        pl.semaphore_signal(barrier, inc=1, device_id=peer, device_id_type=MESH)
    for load in loads[:3]:
        load.wait()
    pl.semaphore_wait(barrier, len(peers))

    q_copies = {}
    mid = nz // 2

    def hop(k):
        for side in range(2):
            held, new = ((nz - k) % nz, nz - k - 1) if side else (k, k + 1)
            first, size, i = 0, rows, new
            if new == mid:
                first, size, i = side * rows // 2, rows // 2, mid + side * (nz - mid)
            q_copies[i] = push(
                q_all.at[rows_of(pos[held] * rows + first, size)],
                q_all.at[rows_of(pos[new] * rows + first, size)],
                q_sem,
                i,
                z_dev(1 if side else nz - 1),
            )

    reached = set()

    def reach(k):
        if k in reached:
            return
        reached.add(k)
        for i in (k, nz if k == mid else nz - k):
            q_copies[i].wait_recv()
        if k < mid:
            hop(k)

    hop(0)

    def shift(lo, size, j, i, device):
        return push(
            cand.at[rows_of(lo, size)],
            cand.at[rows_of(j * shard + lo, size)],
            cand_sem,
            i,
            device,
        )

    cut_at = rows + DIRECT
    y_copies = [
        shift(0, cut_at, 2, 0, y_mate),
        shift(cut_at, shard - cut_at, 2, 1, y_wrap),
    ]
    mate_copy = shift(0, shard, 1, 2, core_mate)

    for load in loads[3:]:
        load.wait()

    def look(i, carry):
        entry = ids_ref[d * rows + i]
        row = tab_ref[pl.ds(lax.shift_right_logical(entry, 7), 1), :]
        lane = lax.broadcasted_iota(jnp.int32, (1, LANES), 1)
        gat[pl.ds(i, 1), :] = jnp.where(lane == (entry & 127), row, 0.0)
        return carry

    lax.fori_loop(0, rows, look, 0, unroll=8)
    offs[0, 0:1, :] = jnp.sum(gat[...].T, axis=0, keepdims=True)
    offs[0, 1 : 1 + neg_rows // LANES, :] = nlq_ref[...]
    off_copies = {}
    for j in (1, 2, 3):
        off_copies[j] = push(
            offs.at[0], offs.at[j], off_sem, j, (g, at(z, j // 2, j % 2))
        )

    eye = lax.broadcasted_iota(jnp.int32, (rows, rows), 0) == lax.broadcasted_iota(
        jnp.int32, (rows, rows), 1
    )
    own = {}

    def prepare(j):
        for k in range(shard // LANES):
            lo = j * shard + k * LANES
            cand_t[:, lo : lo + LANES] = cand[lo : lo + LANES, :].T
        if j:
            off_copies[j].wait_recv()
        for k in range(shard // LANES):
            lo = j * shard + k * LANES
            line = jnp.broadcast_to(offs[j, k : k + 1, :], (LANES, LANES))
            off_b[lo : lo + LANES, :] = line.T

    def score(p, lo, size):
        scaled = q_all[2 * p * rows : (2 * p + 2) * rows, :] * jnp.bfloat16(SCALE)
        ob = off_b[lo : lo + size, :]
        s = dot_nt(cand[lo : lo + size, :], scaled) - jnp.concatenate([ob, ob], axis=1)
        if p == 0 and lo == 0:
            corner = s[:rows, :rows]
            own["score"] = jnp.sum(jnp.where(eye, corner, 0.0), axis=0, keepdims=True)
            corner = jnp.where(eye, MASKED, corner)
            s = jnp.concatenate(
                [jnp.concatenate([corner, s[:rows, rows:]], axis=1), s[rows:]], axis=0
            )
        scores[p, lo : lo + size, :] = s
        return jnp.max(fold(s, jnp.max), axis=0, keepdims=True)

    def weigh(p, lo, size, top):
        total = jnp.zeros((8, 2 * rows), jnp.float32)
        for at_row in range(lo, lo + size, LANES):
            e = jnp.exp(scores[p, at_row : at_row + LANES, :] - top)
            probs[p, at_row : at_row + LANES, :] = e.astype(jnp.bfloat16)
            total = total + fold(e, jnp.sum)
        return jnp.sum(total, axis=0, keepdims=True)

    def pull(p, lo, size):
        return jnp.dot(
            cand_t[:, lo : lo + size],
            probs[p, lo : lo + size, :],
            preferred_element_type=jnp.float32,
        )

    stat_copies = {}

    def tell(p, top, total):
        for h in range(2):
            r = order[2 * p + h]
            lanes = slice(h * rows, (h + 1) * rows)
            both = jnp.concatenate(
                [top[:, lanes], total[:, lanes], jnp.zeros((6, rows), jnp.float32)], axis=0
            )
            if r:
                stat[2 * p + h] = both
                back = nz - r
                stat_copies[back] = push(
                    stat.at[2 * p + h], stat_in.at[back], stat_sem, back, z_dev(r)
                )
            else:
                stat_in[0] = both

    def keep(p, qp):
        for h in range(2):
            part[2 * p + h] = qp[:, h * rows : (h + 1) * rows].astype(jnp.bfloat16)

    half = 2 * shard
    prepare(0)
    mate_copy.wait_recv()
    prepare(1)
    tops, totals, ratios = [], [], []
    for p in range(early):
        reach(p + 1)
        tops.append(score(p, 0, half))
        totals.append(weigh(p, 0, half, tops[p]))
        if p == 0:
            for copy in y_copies:
                copy.wait_recv()
            relay = push(
                cand.at[rows_of(2 * shard, shard)],
                cand.at[rows_of(3 * shard, shard)],
                cand_sem,
                3,
                core_mate,
            )
    prepare(2)
    relay.wait_recv()
    prepare(3)
    for p in range(early):
        top = jnp.maximum(tops[p], score(p, half, half))
        total = weigh(p, half, half, top)
        ratios.append(jnp.exp(tops[p] - top))
        tell(p, top, ratios[p] * totals[p] + total)
        if p == 0 and early < pairs:
            reach(early + 1)
    for p in range(early, pairs):
        reach(p + 1)
        top = score(p, 0, tall)
        total = weigh(p, 0, tall, top)
        tell(p, top, total)
    for p in reversed(range(pairs)):
        if p < early:
            keep(p, ratios[p] * pull(p, 0, half) + pull(p, half, half))
        else:
            keep(p, pull(p, 0, tall))

    for r in range(1, nz):
        stat_copies[r].wait_recv()
    own_score = own["score"]
    best = own_score
    for r in range(nz):
        best = jnp.maximum(best, stat_in[r, 0:1, :])
    mass = jnp.exp(own_score - best)
    for r in range(nz):
        mass = mass + stat_in[r, 1:2, :] * jnp.exp(stat_in[r, 0:1, :] - best)
    log_norm = best + jnp.log(mass)
    lz[...] = jnp.broadcast_to(log_norm, (8, rows))
    lz_copies = {}
    for r in reversed(order):
        if r:
            lz_copies[r] = push(lz, lz_in.at[pos[r]], lz_sem, r, z_dev(nz - r))
    lz_in[pos[0]] = jnp.broadcast_to(log_norm, (8, rows))
    part_copies = {}
    for r in reversed(order):
        if r:
            back = nz - r
            part_copies[back] = push(
                part.at[pos[r]], part_in.at[back], part_sem, back, z_dev(r)
            )
    loss_ref[...] = log_norm - own_score
    own_term = jnp.exp(own_score - log_norm) - 1.0

    def await_lz(p):
        for r in order[2 * p : 2 * p + 2]:
            if r:
                lz_copies[r].wait_recv()

    def again(p, lo, size, lane):
        norm = jnp.concatenate([lz_in[2 * p, 0:1, :], lz_in[2 * p + 1, 0:1, :]], axis=1)

        for at_row in range(lo, lo + size, LANES):
            e = jnp.exp(scores[p, at_row : at_row + LANES, :] - norm)
            probs2[at_row : at_row + LANES, 2 * lane * rows : (2 * lane + 2) * rows] = (
                e.astype(jnp.bfloat16)
            )

    def gather_grad(lo, size, first, last):
        return jnp.dot(
            probs2[lo : lo + size, 0 : 2 * (last - first) * rows],
            q_all[2 * first * rows : 2 * last * rows, :],
            preferred_element_type=jnp.float32,
        )

    if ahead:
        for p in range(ahead):
            await_lz(p)
            again(p, 0, tall, p)
        for j in range(4):
            cgrad[j] = gather_grad(j * shard, shard, 0, ahead)
    for p in range(ahead, pairs):
        await_lz(p)
    d2d_copies = {}
    for j in (3, 1, 2, 0):
        for p in range(ahead, pairs):
            again(p, j * shard, shard, p - ahead)
        grad = gather_grad(j * shard, shard, ahead, pairs)
        if ahead:
            grad = grad + cgrad[j]
        grad = SCALE * grad
        if j in (3, 1):
            i = j // 2
            d2d[i] = grad.astype(jnp.bfloat16)
            d2d_copies[i] = push(d2d.at[i], d2d_in.at[i], d2d_sem, i, core_mate)
        else:
            cgrad[j] = grad

    rs_copies = {}
    for dyl in (1, 0):
        d2d_copies[dyl].wait_recv()
        whole = cgrad[2 * dyl] + d2d_in[dyl].astype(jnp.float32)
        rs[dyl] = whole[rows:].astype(jnp.bfloat16)
        for dyh, dx, dy in far_first:
            if dy == dyl:
                target = grp_at(dyh, dx)
                i = mirror(dyh, dx, dy)
                rs_copies[i] = push(
                    rs.at[dyl, rows_of(pl.multiple_of(target * cut, cut), cut)],
                    rs_in.at[i],
                    rs_sem,
                    i,
                    (target, at(z, dyl, 1)),
                )
        if dyl:
            itm[...] = whole[:rows].astype(jnp.bfloat16)
            itm_copy = push(itm, itm_in, itm_sem, 0, y_mate)
        else:
            cgrad[0] = whole

    own_rows = rows_of(pl.multiple_of(g * cut, cut), cut)
    summed = jnp.zeros((cut, width), jnp.float32)
    for i in range(len(plane)):
        rs_copies[i].wait_recv()
        summed = summed + rs_in[i].astype(jnp.float32)
    red[...] = summed.astype(jnp.bfloat16)
    ag_copies = {}
    for dyh, dx, dyl in far_first:
        if dyl == 0:
            i = mirror(dyh, dx, 0)
            ag_copies[i] = push(
                red, ag.at[own_rows], ag_sem, i, (grp_at(dyh, dx), at(z, 0, 1))
            )

    acc = own_term * cand_t[:, 0:rows].astype(jnp.float32)
    for r in range(nz):
        if r:
            part_copies[r].wait_recv()
            piece = part_in[r]
        else:
            piece = part[pos[0]]
        share = jnp.exp(stat_in[r, 0:1, :] - log_norm)
        acc = acc + share * piece.astype(jnp.float32)
    qg_ref[...] = (SCALE * acc).T

    itm_copy.wait_recv()
    column = jnp.broadcast_to(own_term, (rows, rows)).T
    column = jnp.concatenate([column] * (width // rows), axis=1)
    vg_ref[...] = (
        cgrad[0, 0:rows, :]
        + itm_in[...].astype(jnp.float32)
        + SCALE * column * q_all[0:rows, :].astype(jnp.float32)
    )

    for i in ag_copies:
        ag_copies[i].wait_recv()
    for copy in started:
        copy.wait_send()


def emit(loss_in, qg_in, vg_in, ng_in, loss_ref, qg_ref, vg_ref, ng_ref):
    loss_ref[...] = loss_in[...]
    qg_ref[...] = qg_in[...]
    vg_ref[...] = vg_in[...]
    ng_ref[...] = ng_in[...].astype(jnp.float32)


def local(queries, items, item_ids, neg_embed, neg_logq, logq_table, *, nz, nx):
    rows, width = queries.shape
    neg_rows = neg_embed.shape[0]
    shard = rows + neg_rows
    tall = 4 * shard
    groups = 2 * nx
    cut = neg_rows // groups
    pairs = nz // 2
    f32, bf16 = jnp.float32, jnp.bfloat16
    dma = pltpu.SemaphoreType.DMA
    vmem = pl.BlockSpec(memory_space=pltpu.VMEM)
    away = pl.BlockSpec(memory_space=pl.ANY)
    table = logq_table.reshape(-1, LANES)
    neg_lines = neg_logq.reshape(-1, LANES)
    results = pl.pallas_call(
        functools.partial(kernel, nz, nx),
        out_shape=(
            jax.ShapeDtypeStruct((1, rows), f32),
            jax.ShapeDtypeStruct((rows, width), f32),
            jax.ShapeDtypeStruct((rows, width), f32),
            jax.ShapeDtypeStruct((neg_rows, width), bf16),
        ),
        in_specs=[away] * 6,
        out_specs=(vmem, vmem, vmem, vmem),
        scratch_shapes=[
            pltpu.SMEM(item_ids.shape, jnp.int32),
            pltpu.VMEM(table.shape, f32),
            pltpu.VMEM(neg_lines.shape, f32),
            pltpu.VMEM((nz * rows, width), bf16),
            pltpu.VMEM((tall, width), bf16),
            pltpu.VMEM((width, tall), bf16),
            pltpu.VMEM((4, 8, LANES), f32),
            pltpu.VMEM((tall, LANES), f32),
            pltpu.VMEM((rows, LANES), f32),
            pltpu.VMEM((pairs, tall, 2 * rows), f32),
            pltpu.VMEM((pairs, tall, 2 * rows), bf16),
            pltpu.VMEM((tall, 4 * rows), bf16),
            pltpu.VMEM((4, shard, width), f32),
            pltpu.VMEM((nz, width, rows), bf16),
            pltpu.VMEM((nz, width, rows), bf16),
            pltpu.VMEM((nz, 8, rows), f32),
            pltpu.VMEM((nz, 8, rows), f32),
            pltpu.VMEM((8, rows), f32),
            pltpu.VMEM((nz, 8, rows), f32),
            pltpu.VMEM((2, shard, width), bf16),
            pltpu.VMEM((2, shard, width), bf16),
            pltpu.VMEM((rows, width), bf16),
            pltpu.VMEM((rows, width), bf16),
            pltpu.VMEM((2, neg_rows, width), bf16),
            pltpu.VMEM((2 * groups, cut, width), bf16),
            pltpu.VMEM((cut, width), bf16),
            dma((6,)),
            dma((2, nz + 1)),
            dma((2, 4)),
            dma((2, 4)),
            dma((2, nz)),
            dma((2, nz)),
            dma((2, nz)),
            dma((2, 2)),
            dma((2, 1)),
            dma((2, 2 * groups)),
            dma((2, 2 * groups)),
        ],
        compiler_params=pltpu.CompilerParams(
            collective_id=0, has_side_effects=True, vmem_limit_bytes=60 << 20
        ),
    )(queries, items, item_ids, neg_embed, neg_lines, table)
    loss, qg, vg, ng = pl.pallas_call(
        emit,
        out_shape=(
            jax.ShapeDtypeStruct((1, rows), f32),
            jax.ShapeDtypeStruct((rows, width), f32),
            jax.ShapeDtypeStruct((rows, width), f32),
            jax.ShapeDtypeStruct((neg_rows, width), f32),
        ),
        in_specs=[vmem] * 4,
        out_specs=(vmem, vmem, vmem, vmem),
    )(*results)
    return loss.reshape(rows), qg, vg, ng


def solution(mesh):
    return jax.shard_map(
        functools.partial(
            local, nz=mesh.shape["dev"] // 4, nx=mesh.shape["grp"] // 2
        ),
        mesh=mesh,
        in_specs=(
            P(("grp", "dev"), None),
            P(("grp", "dev"), None),
            P("grp"),
            P("dev", None),
            P("dev"),
            P(),
        ),
        out_specs=(
            P(("grp", "dev")),
            P(("grp", "dev"), None),
            P(("grp", "dev"), None),
            P("dev", None),
        ),
        check_vma=False,
    )
```

time: 67 us -> 59.7 us (0.89)
  local copies, waits for them, and re-layouts: 5.12 us -> 0 us
  Pallas kernels: 60.6 us -> 59 us
    unnamed x6 -> x0, local copies, waits for them, and re-layouts: 5.12 us -> none
    pallas_call x1, Pallas kernels: 60.6 us -> 57 us  [local(): pl.pallas_call(functools.partial(kernel, nz, nx), out_shape=(jax.ShapeDty...]
    pallas_call x0 -> x1, Pallas kernels: none -> 1.98 us  [local(): pl.pallas_call(emit, out_shape=(jax.ShapeDtypeStruct((1, rows), f32), jax...]
where the time goes in v2:
time: 59.7 us; the launch traced here: 59.6 us
  Pallas kernels  59 us (99%)
  between operations  0.64 us (1%)
    pallas_call x1, Pallas kernels, local(): pl.pallas_call(functools.partial(kernel, nz, nx), out_shape=(jax.ShapeDty...  57 us
    pallas_call x1, Pallas kernels, local(): pl.pallas_call(emit, out_shape=(jax.ShapeDtypeStruct((1, rows), f32), jax...  1.98 us

profile of v2, /device:TPU:1, one launch (start us, length us, event | category | flops | bytes accessed | tf_op | source)
XLA Modules:
  0.0 59.6 jit_solution(4470855374642902831)
XLA Ops:
  0.6 57.0 %shard_map.93 = (f32[1,128]{1,0:T(1,128)}, f32[128,256]{1,0:T(8,128)}, f32[128,256]{1,0:T(8,128)}, bf16[512,256]{1,0:T(8,128)(2,1)}) custom-call(bf16[128,256]{1,0:T(8,128)(2,1)} %q_hbm.1, bf16[128,256]{1,0:T(8,128)(2,1)} %v_hbm.1, s32[4096]{0:T(1024)} %ids_hbm.1, bf16[512,256]{1,0:T(8,128)(2,1)} %neg_hbm.1, f32[4,128]{1,0:T(4,128)} %bitcast.4, ...), custom_call_target="tpu_custom_call" | custom-call | tf_op jit(solution)/shard_map/pallas_call | solution.py:495
  57.6 2.0 %shard_map.94 = (f32[1,128]{1,0:T(1,128)}, f32[128,256]{1,0:T(8,128)}, f32[128,256]{1,0:T(8,128)}, f32[512,256]{1,0:T(8,128)}) custom-call(f32[1,128]{1,0:T(1,128)} %get-tuple-element.12.loss_in, f32[128,256]{1,0:T(8,128)} %get-tuple-element.13.qg_in, f32[128,256]{1,0:T(8,128)} %get-tuple-element.14.vg_in, bf16[512,256]{1,0:T(8,128)(2,1)} %get-tuple-element.15.ng_in), custom_call_target="tpu_custom_call" | custom-call | tf_op jit(solution)/shard_map/pallas_call | solution.py:548

commit v3 on v2

--- a/solution.py
+++ b/solution.py
@@ -61,8 +61,6 @@
     part_in,
     stat,
     stat_in,
-    lz,
-    lz_in,
     d2d,
     d2d_in,
     itm,
@@ -75,7 +73,6 @@
     cand_sem,
     off_sem,
     stat_sem,
-    lz_sem,
     part_sem,
     d2d_sem,
     itm_sem,
@@ -163,26 +160,26 @@
     barrier = pltpu.get_barrier_semaphore()
     for peer in peers:
         pl.semaphore_signal(barrier, inc=1, device_id=peer, device_id_type=MESH)
+    pl.semaphore_wait(barrier, len(peers))
     for load in loads[:3]:
         load.wait()
-    pl.semaphore_wait(barrier, len(peers))
 
     q_copies = {}
     mid = nz // 2
-
-    def hop(k):
-        for side in range(2):
-            held, new = ((nz - k) % nz, nz - k - 1) if side else (k, k + 1)
-            first, size, i = 0, rows, new
-            if new == mid:
-                first, size, i = side * rows // 2, rows // 2, mid + side * (nz - mid)
-            q_copies[i] = push(
-                q_all.at[rows_of(pos[held] * rows + first, size)],
-                q_all.at[rows_of(pos[new] * rows + first, size)],
-                q_sem,
-                i,
-                z_dev(1 if side else nz - 1),
-            )
+    direct = min(2, mid)
+
+    def forward(held, step, side):
+        new = (held - step) % nz
+        first, size, i = 0, rows, new
+        if new == mid:
+            first, size, i = side * rows // 2, rows // 2, mid + side * (nz - mid)
+        q_copies[i] = push(
+            q_all.at[rows_of(pos[held] * rows + first, size)],
+            q_all.at[rows_of(pos[new] * rows + first, size)],
+            q_sem,
+            i,
+            z_dev(step % nz),
+        )
 
     reached = set()
 
@@ -192,10 +189,14 @@
         reached.add(k)
         for i in (k, nz if k == mid else nz - k):
             q_copies[i].wait_recv()
-        if k < mid:
-            hop(k)
-
-    hop(0)
+        if k == direct:
+            for far in range(direct + 1, mid + 1):
+                forward(k, k - far, 0)
+                forward(nz - k, far - k, 1)
+
+    for k in range(1, direct + 1):
+        forward(0, -k, 0)
+        forward(0, k, 1)
 
     def shift(lo, size, j, i, device):
         return push(
@@ -277,23 +278,31 @@
             preferred_element_type=jnp.float32,
         )
 
-    stat_copies = {}
+    stat_copies = []
+    far_peers = sorted(range(1, nz), key=lambda r: -min(r, nz - r))
 
     def tell(p, top, total):
-        for h in range(2):
-            r = order[2 * p + h]
-            lanes = slice(h * rows, (h + 1) * rows)
-            both = jnp.concatenate(
-                [top[:, lanes], total[:, lanes], jnp.zeros((6, rows), jnp.float32)], axis=0
+        if p == 0:
+            own["top"] = top[:, :rows]
+            mixed = jnp.maximum(own["top"], own["score"])
+            own_total = total[:, :rows] * jnp.exp(own["top"] - mixed) + jnp.exp(
+                own["score"] - mixed
             )
-            if r:
-                stat[2 * p + h] = both
-                back = nz - r
-                stat_copies[back] = push(
-                    stat.at[2 * p + h], stat_in.at[back], stat_sem, back, z_dev(r)
-                )
-            else:
-                stat_in[0] = both
+            top = jnp.concatenate([mixed, top[:, rows:]], axis=1)
+            total = jnp.concatenate([own_total, total[:, rows:]], axis=1)
+        both = jnp.concatenate([top, total], axis=0)
+        stat[p] = both
+        stat_in[0, p] = both
+        for r in far_peers:
+            s = nz - r
+            stat_copies.append(
+                push(stat.at[p], stat_in.at[s, p], stat_sem, s * pairs + p, z_dev(r))
+            )
+
+    def stats_of(block, s):
+        i = pos[(block - s) % nz]
+        both = stat_in[s, i // 2, :, (i % 2) * rows : (i % 2 + 1) * rows]
+        return both[0:1], both[1:2]
 
     def keep(p, qp):
         for h in range(2):
@@ -309,6 +318,8 @@
         tops.append(score(p, 0, half))
         totals.append(weigh(p, 0, half, tops[p]))
         if p == 0:
+            if early > 1:
+                reach(2)
             for copy in y_copies:
                 copy.wait_recv()
             relay = push(
@@ -339,22 +350,6 @@
         else:
             keep(p, pull(p, 0, tall))
 
-    for r in range(1, nz):
-        stat_copies[r].wait_recv()
-    own_score = own["score"]
-    best = own_score
-    for r in range(nz):
-        best = jnp.maximum(best, stat_in[r, 0:1, :])
-    mass = jnp.exp(own_score - best)
-    for r in range(nz):
-        mass = mass + stat_in[r, 1:2, :] * jnp.exp(stat_in[r, 0:1, :] - best)
-    log_norm = best + jnp.log(mass)
-    lz[...] = jnp.broadcast_to(log_norm, (8, rows))
-    lz_copies = {}
-    for r in reversed(order):
-        if r:
-            lz_copies[r] = push(lz, lz_in.at[pos[r]], lz_sem, r, z_dev(nz - r))
-    lz_in[pos[0]] = jnp.broadcast_to(log_norm, (8, rows))
     part_copies = {}
     for r in reversed(order):
         if r:
@@ -362,57 +357,36 @@
             part_copies[back] = push(
                 part.at[pos[r]], part_in.at[back], part_sem, back, z_dev(r)
             )
+    for copy in stat_copies:
+        copy.wait_recv()
+    own_score = own["score"]
+    norms = []
+    for r in order:
+        tops_r, totals_r = zip(*(stats_of(r, s) for s in range(nz)))
+        tops_r = jnp.concatenate(tops_r, axis=0)
+        totals_r = jnp.concatenate(totals_r, axis=0)
+        best = jnp.max(tops_r, axis=0, keepdims=True)
+        mass = jnp.sum(totals_r * jnp.exp(tops_r - best), axis=0, keepdims=True)
+        norms.append(best + jnp.log(mass))
+    log_norm = norms[pos[0]]
     loss_ref[...] = log_norm - own_score
     own_term = jnp.exp(own_score - log_norm) - 1.0
 
-    def await_lz(p):
-        for r in order[2 * p : 2 * p + 2]:
-            if r:
-                lz_copies[r].wait_recv()
-
-    def again(p, lo, size, lane):
-        norm = jnp.concatenate([lz_in[2 * p, 0:1, :], lz_in[2 * p + 1, 0:1, :]], axis=1)
-
-        for at_row in range(lo, lo + size, LANES):
-            e = jnp.exp(scores[p, at_row : at_row + LANES, :] - norm)
-            probs2[at_row : at_row + LANES, 2 * lane * rows : (2 * lane + 2) * rows] = (
-                e.astype(jnp.bfloat16)
-            )
-
-    def gather_grad(lo, size, first, last):
-        return jnp.dot(
-            probs2[lo : lo + size, 0 : 2 * (last - first) * rows],
-            q_all[2 * first * rows : 2 * last * rows, :],
-            preferred_element_type=jnp.float32,
-        )
-
-    if ahead:
-        for p in range(ahead):
-            await_lz(p)
-            again(p, 0, tall, p)
-        for j in range(4):
-            cgrad[j] = gather_grad(j * shard, shard, 0, ahead)
-    for p in range(ahead, pairs):
-        await_lz(p)
-    d2d_copies = {}
-    for j in (3, 1, 2, 0):
-        for p in range(ahead, pairs):
-            again(p, j * shard, shard, p - ahead)
-        grad = gather_grad(j * shard, shard, ahead, pairs)
-        if ahead:
-            grad = grad + cgrad[j]
-        grad = SCALE * grad
-        if j in (3, 1):
-            i = j // 2
-            d2d[i] = grad.astype(jnp.bfloat16)
-            d2d_copies[i] = push(d2d.at[i], d2d_in.at[i], d2d_sem, i, core_mate)
-        else:
-            cgrad[j] = grad
-
-    rs_copies = {}
-    for dyl in (1, 0):
+    def weigh_again(j, slot):
+        for p in range(pairs):
+            norm = jnp.concatenate(norms[2 * p : 2 * p + 2], axis=1)
+            for lo in range(0, shard, LANES):
+                at_row = j * shard + lo
+                e = jnp.exp(scores[p, at_row : at_row + LANES, :] - norm)
+                probs2[slot, lo : lo + LANES, 2 * p * rows : (2 * p + 2) * rows] = (
+                    e.astype(jnp.bfloat16)
+                )
+
+    d2d_copies, rs_copies = {}, {}
+
+    def exchange(dyl):
         d2d_copies[dyl].wait_recv()
-        whole = cgrad[2 * dyl] + d2d_in[dyl].astype(jnp.float32)
+        whole = cgrad[dyl] + d2d_in[dyl].astype(jnp.float32)
         rs[dyl] = whole[rows:].astype(jnp.bfloat16)
         for dyh, dx, dy in far_first:
             if dy == dyl:
@@ -427,9 +401,23 @@
                 )
         if dyl:
             itm[...] = whole[:rows].astype(jnp.bfloat16)
-            itm_copy = push(itm, itm_in, itm_sem, 0, y_mate)
+            return push(itm, itm_in, itm_sem, 0, y_mate)
+        cgrad[0, 0:rows, :] = whole[:rows]
+
+    for turn, j in enumerate((3, 2, 1, 0)):
+        weigh_again(j, turn % 2)
+        grad = SCALE * jnp.dot(
+            probs2[turn % 2], q_all[...], preferred_element_type=jnp.float32
+        )
+        if j % 2:
+            i = j // 2
+            d2d[i] = grad.astype(jnp.bfloat16)
+            d2d_copies[i] = push(d2d.at[i], d2d_in.at[i], d2d_sem, i, core_mate)
         else:
-            cgrad[0] = whole
+            cgrad[j // 2] = grad
+        if j == 1:
+            itm_copy = exchange(1)
+    exchange(0)
 
     own_rows = rows_of(pl.multiple_of(g * cut, cut), cut)
     summed = jnp.zeros((cut, width), jnp.float32)
@@ -452,7 +440,7 @@
             piece = part_in[r]
         else:
             piece = part[pos[0]]
-        share = jnp.exp(stat_in[r, 0:1, :] - log_norm)
+        share = jnp.exp((stats_of(0, r)[0] if r else own["top"]) - log_norm)
         acc = acc + share * piece.astype(jnp.float32)
     qg_ref[...] = (SCALE * acc).T
 
@@ -514,14 +502,12 @@
             pltpu.VMEM((rows, LANES), f32),
             pltpu.VMEM((pairs, tall, 2 * rows), f32),
             pltpu.VMEM((pairs, tall, 2 * rows), bf16),
-            pltpu.VMEM((tall, 4 * rows), bf16),
-            pltpu.VMEM((4, shard, width), f32),
+            pltpu.VMEM((2, shard, nz * rows), bf16),
+            pltpu.VMEM((2, shard, width), f32),
             pltpu.VMEM((nz, width, rows), bf16),
             pltpu.VMEM((nz, width, rows), bf16),
-            pltpu.VMEM((nz, 8, rows), f32),
-            pltpu.VMEM((nz, 8, rows), f32),
-            pltpu.VMEM((8, rows), f32),
-            pltpu.VMEM((nz, 8, rows), f32),
+            pltpu.VMEM((pairs, 2, 2 * rows), f32),
+            pltpu.VMEM((nz, pairs, 2, 2 * rows), f32),
             pltpu.VMEM((2, shard, width), bf16),
             pltpu.VMEM((2, shard, width), bf16),
             pltpu.VMEM((rows, width), bf16),
@@ -533,8 +519,7 @@
             dma((2, nz + 1)),
             dma((2, 4)),
             dma((2, 4)),
-            dma((2, nz)),
-            dma((2, nz)),
+            dma((2, nz * pairs)),
             dma((2, nz)),
             dma((2, 2)),
             dma((2, 1)),

time: 59.7 us -> 53.7 us (0.90)
  Pallas kernels: 59 us -> 53 us
    pallas_call x1, Pallas kernels: 57 us -> 51 us  [local(): pl.pallas_call(functools.partial(kernel, nz, nx), out_shape=(jax.ShapeDty...]
where the time goes in v3:
time: 53.7 us; the launch traced here: 53.6 us
  Pallas kernels  53 us (99%)
  between operations  0.64 us (1%)
    pallas_call x1, Pallas kernels, local(): pl.pallas_call(functools.partial(kernel, nz, nx), out_shape=(jax.ShapeDty...  51 us
    pallas_call x1, Pallas kernels, local(): pl.pallas_call(emit, out_shape=(jax.ShapeDtypeStruct((1, rows), f32), jax...  1.98 us

profile of v3, /device:TPU:1, one launch (start us, length us, event | category | flops | bytes accessed | tf_op | source)
XLA Modules:
  0.0 53.6 jit_solution(17460317033649485223)
XLA Ops:
  0.6 51.0 %shard_map.93 = (f32[1,128]{1,0:T(1,128)}, f32[128,256]{1,0:T(8,128)}, f32[128,256]{1,0:T(8,128)}, bf16[512,256]{1,0:T(8,128)(2,1)}) custom-call(bf16[128,256]{1,0:T(8,128)(2,1)} %q_hbm.1, bf16[128,256]{1,0:T(8,128)(2,1)} %v_hbm.1, s32[4096]{0:T(1024)} %ids_hbm.1, bf16[512,256]{1,0:T(8,128)(2,1)} %neg_hbm.1, f32[4,128]{1,0:T(4,128)} %bitcast.4, ...), custom_call_target="tpu_custom_call" | custom-call | tf_op jit(solution)/shard_map/pallas_call | solution.py:483
  51.6 2.0 %shard_map.94 = (f32[1,128]{1,0:T(1,128)}, f32[128,256]{1,0:T(8,128)}, f32[128,256]{1,0:T(8,128)}, f32[512,256]{1,0:T(8,128)}) custom-call(f32[1,128]{1,0:T(1,128)} %get-tuple-element.12.loss_in, f32[128,256]{1,0:T(8,128)} %get-tuple-element.13.qg_in, f32[128,256]{1,0:T(8,128)} %get-tuple-element.14.vg_in, bf16[512,256]{1,0:T(8,128)(2,1)} %get-tuple-element.15.ng_in), custom_call_target="tpu_custom_call" | custom-call | tf_op jit(solution)/shard_map/pallas_call | solution.py:533

commit v4 on v3

--- a/solution.py
+++ b/solution.py
@@ -88,9 +88,7 @@
     cut = neg_rows // groups
     order = pair_order(nz)
     pos = {r: i for i, r in enumerate(order)}
-    pairs = nz // 2
-    early = max(1, pairs // 2)
-    ahead = max(0, pairs - 2)
+    pairs = mid = nz // 2
 
     g = lax.axis_index("grp")
     d = lax.axis_index("dev")
@@ -104,7 +102,8 @@
         return ((yh + dyh) % 2) * nx + (x + dx) % nx
 
     def z_dev(r):
-        return (g, at((z + r) % nz, 0, r))
+        zz = (z + r) % nz
+        return (g, at(zz, 0, z + zz + z // mid + zz // mid))
 
     def distance(dyh, dx, dyl):
         return min(dx, nx - dx) + (1 if dyl else 2 * dyh)
@@ -165,7 +164,6 @@
         load.wait()
 
     q_copies = {}
-    mid = nz // 2
     direct = min(2, mid)
 
     def forward(held, step, side):
@@ -251,17 +249,22 @@
 
     def score(p, lo, size):
         scaled = q_all[2 * p * rows : (2 * p + 2) * rows, :] * jnp.bfloat16(SCALE)
-        ob = off_b[lo : lo + size, :]
-        s = dot_nt(cand[lo : lo + size, :], scaled) - jnp.concatenate([ob, ob], axis=1)
-        if p == 0 and lo == 0:
-            corner = s[:rows, :rows]
-            own["score"] = jnp.sum(jnp.where(eye, corner, 0.0), axis=0, keepdims=True)
-            corner = jnp.where(eye, MASKED, corner)
-            s = jnp.concatenate(
-                [jnp.concatenate([corner, s[:rows, rows:]], axis=1), s[rows:]], axis=0
-            )
-        scores[p, lo : lo + size, :] = s
-        return jnp.max(fold(s, jnp.max), axis=0, keepdims=True)
+        top = jnp.full((8, 2 * rows), MASKED, jnp.float32)
+        for at_row in range(lo, lo + size, 256):
+            ob = off_b[at_row : at_row + 256, :]
+            s = dot_nt(cand[at_row : at_row + 256, :], scaled)
+            s = s - jnp.concatenate([ob, ob], axis=1)
+            if p == 0 and at_row == 0:
+                corner = s[:rows, :rows]
+                own["score"] = jnp.sum(
+                    jnp.where(eye, corner, 0.0), axis=0, keepdims=True
+                )
+                corner = jnp.where(eye, MASKED, corner)
+                line = jnp.concatenate([corner, s[:rows, rows:]], axis=1)
+                s = jnp.concatenate([line, s[rows:]], axis=0) if 256 > rows else line
+            scores[p, at_row : at_row + 256, :] = s
+            top = jnp.maximum(top, fold(s, jnp.max))
+        return jnp.max(top, axis=0, keepdims=True)
 
     def weigh(p, lo, size, top):
         total = jnp.zeros((8, 2 * rows), jnp.float32)
@@ -312,44 +315,40 @@
     prepare(0)
     mate_copy.wait_recv()
     prepare(1)
-    tops, totals, ratios = [], [], []
-    for p in range(early):
-        reach(p + 1)
-        tops.append(score(p, 0, half))
-        totals.append(weigh(p, 0, half, tops[p]))
-        if p == 0:
-            if early > 1:
-                reach(2)
-            for copy in y_copies:
-                copy.wait_recv()
-            relay = push(
-                cand.at[rows_of(2 * shard, shard)],
-                cand.at[rows_of(3 * shard, shard)],
-                cand_sem,
-                3,
-                core_mate,
-            )
+    reach(1)
+    first_top = score(0, 0, half)
+    first_total = weigh(0, 0, half, first_top)
+    for copy in y_copies:
+        copy.wait_recv()
+    relay = push(
+        cand.at[rows_of(2 * shard, shard)],
+        cand.at[rows_of(3 * shard, shard)],
+        cand_sem,
+        3,
+        core_mate,
+    )
     prepare(2)
+    if pairs > 1:
+        reach(2)
     relay.wait_recv()
     prepare(3)
-    for p in range(early):
-        top = jnp.maximum(tops[p], score(p, half, half))
-        total = weigh(p, half, half, top)
-        ratios.append(jnp.exp(tops[p] - top))
-        tell(p, top, ratios[p] * totals[p] + total)
-        if p == 0 and early < pairs:
-            reach(early + 1)
-    for p in range(early, pairs):
+    top = jnp.maximum(first_top, score(0, half, half))
+    total = weigh(0, half, half, top)
+    ratio = jnp.exp(first_top - top)
+    tell(0, top, ratio * first_total + total)
+    for p in range(1, pairs):
         reach(p + 1)
         top = score(p, 0, tall)
         total = weigh(p, 0, tall, top)
         tell(p, top, total)
     for p in reversed(range(pairs)):
-        if p < early:
-            keep(p, ratios[p] * pull(p, 0, half) + pull(p, half, half))
+        if p:
+            keep(p, pull(p, 0, tall))
         else:
-            keep(p, pull(p, 0, tall))
-
+            keep(p, ratio * pull(p, 0, half) + pull(p, half, half))
+
+    for copy in stat_copies:
+        copy.wait_recv()
     part_copies = {}
     for r in reversed(order):
         if r:
@@ -357,8 +356,6 @@
             part_copies[back] = push(
                 part.at[pos[r]], part_in.at[back], part_sem, back, z_dev(r)
             )
-    for copy in stat_copies:
-        copy.wait_recv()
     own_score = own["score"]
     norms = []
     for r in order:
@@ -459,11 +456,23 @@
         copy.wait_send()
 
 
-def emit(loss_in, qg_in, vg_in, ng_in, loss_ref, qg_ref, vg_ref, ng_ref):
-    loss_ref[...] = loss_in[...]
-    qg_ref[...] = qg_in[...]
-    vg_ref[...] = vg_in[...]
-    ng_ref[...] = ng_in[...].astype(jnp.float32)
+def emit(loss_in, qg_in, vg_in, ng_in, loss, qg, vg, ng, wide, sem):
+    copies = [
+        pltpu.make_async_copy(qg_in, qg, sem.at[0]),
+        pltpu.make_async_copy(vg_in, vg, sem.at[1]),
+        pltpu.make_async_copy(loss_in, loss, sem.at[2]),
+    ]
+    for copy in copies:
+        copy.start()
+    size = ng_in.shape[0] // 2
+    for i in range(2):
+        span = pl.ds(i * size, size)
+        wide[span, :] = ng_in[span, :].astype(jnp.float32)
+        copy = pltpu.make_async_copy(wide.at[span], ng.at[span], sem.at[3 + i])
+        copy.start()
+        copies.append(copy)
+    for copy in copies:
+        copy.wait()
 
 
 def local(queries, items, item_ids, neg_embed, neg_logq, logq_table, *, nz, nx):
@@ -483,10 +492,10 @@
     results = pl.pallas_call(
         functools.partial(kernel, nz, nx),
         out_shape=(
-            jax.ShapeDtypeStruct((1, rows), f32),
-            jax.ShapeDtypeStruct((rows, width), f32),
-            jax.ShapeDtypeStruct((rows, width), f32),
-            jax.ShapeDtypeStruct((neg_rows, width), bf16),
+            pltpu.VMEM((1, rows), f32),
+            pltpu.VMEM((rows, width), f32),
+            pltpu.VMEM((rows, width), f32),
+            pltpu.VMEM((neg_rows, width), bf16),
         ),
         in_specs=[away] * 6,
         out_specs=(vmem, vmem, vmem, vmem),
@@ -539,8 +548,9 @@
             jax.ShapeDtypeStruct((neg_rows, width), f32),
         ),
         in_specs=[vmem] * 4,
-        out_specs=(vmem, vmem, vmem, vmem),
-    )(*results)
+        out_specs=(away, away, away, away),
+        scratch_shapes=[pltpu.VMEM((neg_rows, width), f32), dma((5,))],
+    )(*(pltpu.with_memory_space_constraint(r, pltpu.VMEM) for r in results))
     return loss.reshape(rows), qg, vg, ng
 
 

time: 53.7 us -> 50.4 us (0.939)
  Pallas kernels: 53 us -> 49.7 us
    pallas_call x1, Pallas kernels: 51 us -> 48.8 us  [local(): pl.pallas_call(functools.partial(kernel, nz, nx), out_shape=(pltpu.VMEM((...]
    pallas_call x1, Pallas kernels: 1.98 us -> 0.93 us  [local(): pl.pallas_call(emit, out_shape=(jax.ShapeDtypeStruct((1, rows), f32), jax...]
where the time goes in v4:
time: 50.4 us; the launch traced here: 50.3 us
  Pallas kernels  49.7 us (99%)
  between operations  0.64 us (1%)
    pallas_call x1, Pallas kernels, local(): pl.pallas_call(functools.partial(kernel, nz, nx), out_shape=(pltpu.VMEM((...  48.8 us

profile of v4, /device:TPU:1, one launch (start us, length us, event | category | flops | bytes accessed | tf_op | source)
XLA Modules:
  0.0 50.3 jit_solution(17294143980678934630)
XLA Ops:
  0.6 48.8 %shard_map.93 = (f32[1,128]{1,0:T(1,128)S(1)}, f32[128,256]{1,0:T(8,128)S(1)}, f32[128,256]{1,0:T(8,128)S(1)}, bf16[512,256]{1,0:T(8,128)(2,1)S(1)}) custom-call(bf16[128,256]{1,0:T(8,128)(2,1)} %q_hbm.1, bf16[128,256]{1,0:T(8,128)(2,1)} %v_hbm.1, s32[4096]{0:T(1024)} %ids_hbm.1, bf16[512,256]{1,0:T(8,128)(2,1)} %neg_hbm.1, f32[4,128]{1,0:T(4,128)} %bitcast.4, ...), custom_call_target="tpu_custom_call" | custom-call | tf_op jit(solution)/shard_map/pallas_call | solution.py:492
  49.4 0.9 %shard_map.94 = (f32[1,128]{1,0:T(1,128)}, f32[128,256]{1,0:T(8,128)}, f32[128,256]{1,0:T(8,128)}, f32[512,256]{1,0:T(8,128)}) custom-call(f32[1,128]{1,0:T(1,128)S(1)} %get-tuple-element.12.loss_in, f32[128,256]{1,0:T(8,128)S(1)} %get-tuple-element.13.qg_in, f32[128,256]{1,0:T(8,128)S(1)} %get-tuple-element.14.vg_in, ...), custom_call_target="tpu_custom_call" | custom-call | tf_op jit(solution)/shard_map/pallas_call | solution.py:542

commit v5 on v4

--- a/solution.py
+++ b/solution.py
@@ -15,9 +15,9 @@
 
 
 def pair_order(nz):
-    order = [0, 1]
+    order = [0, nz // 2]
     for r in range(1, nz // 2):
-        order += [nz - r, r + 1]
+        order += [r, nz - r]
     return order
 
 
@@ -55,7 +55,6 @@
     gat,
     scores,
     probs,
-    probs2,
     cgrad,
     part,
     part_in,
@@ -134,16 +133,8 @@
     def rows_of(start, size):
         return pl.ds(start, size)
 
-    loads = [
-        pltpu.make_async_copy(q_hbm, q_all.at[rows_of(0, rows)], in_sem.at[0]),
-        pltpu.make_async_copy(v_hbm, cand.at[rows_of(0, rows)], in_sem.at[1]),
-        pltpu.make_async_copy(neg_hbm, cand.at[rows_of(rows, neg_rows)], in_sem.at[2]),
-        pltpu.make_async_copy(ids_hbm, ids_ref, in_sem.at[3]),
-        pltpu.make_async_copy(tab_hbm, tab_ref, in_sem.at[4]),
-        pltpu.make_async_copy(nlq_hbm, nlq_ref, in_sem.at[5]),
-    ]
-    for load in loads:
-        load.start()
+    def lanes_of(p):
+        return slice(2 * p * rows, (2 * p + 2) * rows)
 
     core_mate = (g, at(z, 0, 1))
     y_mate = (g, at(z, 1, 0))
@@ -159,6 +150,16 @@
     barrier = pltpu.get_barrier_semaphore()
     for peer in peers:
         pl.semaphore_signal(barrier, inc=1, device_id=peer, device_id_type=MESH)
+    loads = [
+        pltpu.make_async_copy(q_hbm, q_all.at[rows_of(0, rows)], in_sem.at[0]),
+        pltpu.make_async_copy(v_hbm, cand.at[rows_of(0, rows)], in_sem.at[1]),
+        pltpu.make_async_copy(neg_hbm, cand.at[rows_of(rows, neg_rows)], in_sem.at[2]),
+        pltpu.make_async_copy(ids_hbm, ids_ref, in_sem.at[3]),
+        pltpu.make_async_copy(tab_hbm, tab_ref, in_sem.at[4]),
+        pltpu.make_async_copy(nlq_hbm, nlq_ref, in_sem.at[5]),
+    ]
+    for load in loads:
+        load.start()
     pl.semaphore_wait(barrier, len(peers))
     for load in loads[:3]:
         load.wait()
@@ -188,11 +189,11 @@
         for i in (k, nz if k == mid else nz - k):
             q_copies[i].wait_recv()
         if k == direct:
-            for far in range(direct + 1, mid + 1):
+            for far in range(3, mid + 1):
                 forward(k, k - far, 0)
                 forward(nz - k, far - k, 1)
 
-    for k in range(1, direct + 1):
+    for k in [k for k in (2, 1) if k <= mid]:
         forward(0, -k, 0)
         forward(0, k, 1)
 
@@ -270,18 +271,18 @@
         total = jnp.zeros((8, 2 * rows), jnp.float32)
         for at_row in range(lo, lo + size, LANES):
             e = jnp.exp(scores[p, at_row : at_row + LANES, :] - top)
-            probs[p, at_row : at_row + LANES, :] = e.astype(jnp.bfloat16)
+            probs[at_row : at_row + LANES, lanes_of(p)] = e.astype(jnp.bfloat16)
             total = total + fold(e, jnp.sum)
         return jnp.sum(total, axis=0, keepdims=True)
 
     def pull(p, lo, size):
         return jnp.dot(
             cand_t[:, lo : lo + size],
-            probs[p, lo : lo + size, :],
+            probs[lo : lo + size, lanes_of(p)],
             preferred_element_type=jnp.float32,
         )
 
-    stat_copies = []
+    stat_copies = {}
     far_peers = sorted(range(1, nz), key=lambda r: -min(r, nz - r))
 
     def tell(p, top, total):
@@ -298,8 +299,8 @@
         stat_in[0, p] = both
         for r in far_peers:
             s = nz - r
-            stat_copies.append(
-                push(stat.at[p], stat_in.at[s, p], stat_sem, s * pairs + p, z_dev(r))
+            stat_copies[s, p] = push(
+                stat.at[p], stat_in.at[s, p], stat_sem, s * pairs + p, z_dev(r)
             )
 
     def stats_of(block, s):
@@ -315,9 +316,11 @@
     prepare(0)
     mate_copy.wait_recv()
     prepare(1)
-    reach(1)
-    first_top = score(0, 0, half)
-    first_total = weigh(0, 0, half, first_top)
+    turns = [p for p in (2, 1, 3) if p < pairs] + [0]
+    lead = turns[0]
+    reach(lead or mid)
+    first_top = score(lead, 0, half)
+    first_total = weigh(lead, 0, half, first_top)
     for copy in y_copies:
         copy.wait_recv()
     relay = push(
@@ -328,27 +331,53 @@
         core_mate,
     )
     prepare(2)
-    if pairs > 1:
-        reach(2)
     relay.wait_recv()
     prepare(3)
-    top = jnp.maximum(first_top, score(0, half, half))
-    total = weigh(0, half, half, top)
+    top = jnp.maximum(first_top, score(lead, half, half))
+    total = weigh(lead, half, half, top)
     ratio = jnp.exp(first_top - top)
-    tell(0, top, ratio * first_total + total)
-    for p in range(1, pairs):
-        reach(p + 1)
+    tell(lead, top, ratio * first_total + total)
+    for p in turns[1:]:
+        reach(p or mid)
         top = score(p, 0, tall)
         total = weigh(p, 0, tall, top)
         tell(p, top, total)
     for p in reversed(range(pairs)):
-        if p:
+        if p != lead:
             keep(p, pull(p, 0, tall))
         else:
             keep(p, ratio * pull(p, 0, half) + pull(p, half, half))
 
-    for copy in stat_copies:
-        copy.wait_recv()
+    own_score = own["score"]
+    norms = {}
+
+    def settle(p):
+        for r in order[2 * p : 2 * p + 2]:
+            for s in range(1, nz):
+                copy = stat_copies.pop((s, pos[(r - s) % nz] // 2), None)
+                if copy is not None:
+                    copy.wait_recv()
+        for r in order[2 * p : 2 * p + 2]:
+            tops_r, totals_r = zip(*(stats_of(r, s) for s in range(nz)))
+            tops_r = jnp.concatenate(tops_r, axis=0)
+            totals_r = jnp.concatenate(totals_r, axis=0)
+            best = jnp.max(tops_r, axis=0, keepdims=True)
+            mass = jnp.sum(totals_r * jnp.exp(tops_r - best), axis=0, keepdims=True)
+            norms[r] = best + jnp.log(mass)
+
+    def weigh_again(p, first, last):
+        norm = jnp.concatenate([norms[r] for r in order[2 * p : 2 * p + 2]], axis=1)
+        for at_row in range(first * shard, last * shard, LANES):
+            e = jnp.exp(scores[p, at_row : at_row + LANES, :] - norm)
+            probs[at_row : at_row + LANES, lanes_of(p)] = e.astype(jnp.bfloat16)
+
+    sooner = [p for p in (2, 3) if p < pairs]
+    later = [p for p in (1, 0) if p < pairs]
+    for p in sooner:
+        settle(p)
+        weigh_again(p, 0, 4)
+    for p in later:
+        settle(p)
     part_copies = {}
     for r in reversed(order):
         if r:
@@ -356,28 +385,9 @@
             part_copies[back] = push(
                 part.at[pos[r]], part_in.at[back], part_sem, back, z_dev(r)
             )
-    own_score = own["score"]
-    norms = []
-    for r in order:
-        tops_r, totals_r = zip(*(stats_of(r, s) for s in range(nz)))
-        tops_r = jnp.concatenate(tops_r, axis=0)
-        totals_r = jnp.concatenate(totals_r, axis=0)
-        best = jnp.max(tops_r, axis=0, keepdims=True)
-        mass = jnp.sum(totals_r * jnp.exp(tops_r - best), axis=0, keepdims=True)
-        norms.append(best + jnp.log(mass))
-    log_norm = norms[pos[0]]
+    log_norm = norms[0]
     loss_ref[...] = log_norm - own_score
     own_term = jnp.exp(own_score - log_norm) - 1.0
-
-    def weigh_again(j, slot):
-        for p in range(pairs):
-            norm = jnp.concatenate(norms[2 * p : 2 * p + 2], axis=1)
-            for lo in range(0, shard, LANES):
-                at_row = j * shard + lo
-                e = jnp.exp(scores[p, at_row : at_row + LANES, :] - norm)
-                probs2[slot, lo : lo + LANES, 2 * p * rows : (2 * p + 2) * rows] = (
-                    e.astype(jnp.bfloat16)
-                )
 
     d2d_copies, rs_copies = {}, {}
 
@@ -401,18 +411,22 @@
             return push(itm, itm_in, itm_sem, 0, y_mate)
         cgrad[0, 0:rows, :] = whole[:rows]
 
-    for turn, j in enumerate((3, 2, 1, 0)):
-        weigh_again(j, turn % 2)
-        grad = SCALE * jnp.dot(
-            probs2[turn % 2], q_all[...], preferred_element_type=jnp.float32
+    for j in (3, 1, 2, 0):
+        for p in later:
+            weigh_again(p, j, j + 1)
+        grad = jnp.dot(
+            probs[j * shard : (j + 1) * shard, :],
+            q_all[...],
+            preferred_element_type=jnp.float32,
         )
+        grad = SCALE * grad
         if j % 2:
             i = j // 2
             d2d[i] = grad.astype(jnp.bfloat16)
             d2d_copies[i] = push(d2d.at[i], d2d_in.at[i], d2d_sem, i, core_mate)
         else:
             cgrad[j // 2] = grad
-        if j == 1:
+        if j == 2:
             itm_copy = exchange(1)
     exchange(0)
 
@@ -510,8 +524,7 @@
             pltpu.VMEM((tall, LANES), f32),
             pltpu.VMEM((rows, LANES), f32),
             pltpu.VMEM((pairs, tall, 2 * rows), f32),
-            pltpu.VMEM((pairs, tall, 2 * rows), bf16),
-            pltpu.VMEM((2, shard, nz * rows), bf16),
+            pltpu.VMEM((tall, nz * rows), bf16),
             pltpu.VMEM((2, shard, width), f32),
             pltpu.VMEM((nz, width, rows), bf16),
             pltpu.VMEM((nz, width, rows), bf16),

time: 50.4 us -> 49.4 us (0.980)
  Pallas kernels: 49.7 us -> 48.7 us
    pallas_call x1, Pallas kernels: 48.8 us -> 47.8 us  [local(): pl.pallas_call(functools.partial(kernel, nz, nx), out_shape=(pltpu.VMEM((...]
where the time goes in v5:
time: 49.4 us; the launch traced here: 49.3 us
  Pallas kernels  48.7 us (99%)
  between operations  0.64 us (1%)
    pallas_call x1, Pallas kernels, local(): pl.pallas_call(functools.partial(kernel, nz, nx), out_shape=(pltpu.VMEM((...  47.8 us

profile of v5, /device:TPU:1, one launch (start us, length us, event | category | flops | bytes accessed | tf_op | source)
XLA Modules:
  0.0 49.3 jit_solution(4009529466029512857)
XLA Ops:
  0.6 47.8 %shard_map.93 = (f32[1,128]{1,0:T(1,128)S(1)}, f32[128,256]{1,0:T(8,128)S(1)}, f32[128,256]{1,0:T(8,128)S(1)}, bf16[512,256]{1,0:T(8,128)(2,1)S(1)}) custom-call(bf16[128,256]{1,0:T(8,128)(2,1)} %q_hbm.1, bf16[128,256]{1,0:T(8,128)(2,1)} %v_hbm.1, s32[4096]{0:T(1024)} %ids_hbm.1, bf16[512,256]{1,0:T(8,128)(2,1)} %neg_hbm.1, f32[4,128]{1,0:T(4,128)} %bitcast.4, ...), custom_call_target="tpu_custom_call" | custom-call | tf_op jit(solution)/shard_map/pallas_call | solution.py:506
  48.4 0.9 %shard_map.94 = (f32[1,128]{1,0:T(1,128)}, f32[128,256]{1,0:T(8,128)}, f32[128,256]{1,0:T(8,128)}, f32[512,256]{1,0:T(8,128)}) custom-call(f32[1,128]{1,0:T(1,128)S(1)} %get-tuple-element.12.loss_in, f32[128,256]{1,0:T(8,128)S(1)} %get-tuple-element.13.qg_in, f32[128,256]{1,0:T(8,128)S(1)} %get-tuple-element.14.vg_in, ...), custom_call_target="tpu_custom_call" | custom-call | tf_op jit(solution)/shard_map/pallas_call | solution.py:555

commit v6 on v5

--- a/solution.py
+++ b/solution.py
@@ -237,10 +237,12 @@
     )
     own = {}
 
-    def prepare(j):
+    def flip(j):
         for k in range(shard // LANES):
             lo = j * shard + k * LANES
             cand_t[:, lo : lo + LANES] = cand[lo : lo + LANES, :].T
+
+    def spread(j):
         if j:
             off_copies[j].wait_recv()
         for k in range(shard // LANES):
@@ -313,14 +315,22 @@
             part[2 * p + h] = qp[:, h * rows : (h + 1) * rows].astype(jnp.bfloat16)
 
     half = 2 * shard
-    prepare(0)
+    spread(0)
+    flip(0)
     mate_copy.wait_recv()
-    prepare(1)
+    flip(1)
+    for j in (1, 2, 3):
+        spread(j)
     turns = [p for p in (2, 1, 3) if p < pairs] + [0]
-    lead = turns[0]
-    reach(lead or mid)
-    first_top = score(lead, 0, half)
-    first_total = weigh(lead, 0, half, first_top)
+    split = turns[: 2 if pairs > 2 else 1]
+    tops, totals, ratios = {}, {}, {}
+
+    def first_round(p):
+        reach(p or mid)
+        tops[p] = score(p, 0, half)
+        totals[p] = weigh(p, 0, half, tops[p])
+
+    first_round(split[0])
     for copy in y_copies:
         copy.wait_recv()
     relay = push(
@@ -330,24 +340,34 @@
         3,
         core_mate,
     )
-    prepare(2)
+    for p in split[1:]:
+        first_round(p)
     relay.wait_recv()
-    prepare(3)
-    top = jnp.maximum(first_top, score(lead, half, half))
-    total = weigh(lead, half, half, top)
-    ratio = jnp.exp(first_top - top)
-    tell(lead, top, ratio * first_total + total)
-    for p in turns[1:]:
+    for p in split:
+        top = jnp.maximum(tops[p], score(p, half, half))
+        total = weigh(p, half, half, top)
+        ratios[p] = jnp.exp(tops[p] - top)
+        tell(p, top, ratios[p] * totals[p] + total)
+    for p in turns[len(split) :]:
         reach(p or mid)
         top = score(p, 0, tall)
         total = weigh(p, 0, tall, top)
         tell(p, top, total)
-    for p in reversed(range(pairs)):
-        if p != lead:
+    flip(2)
+    flip(3)
+    for p in range(pairs):
+        if p in split:
+            keep(p, ratios[p] * pull(p, 0, half) + pull(p, half, half))
+        else:
             keep(p, pull(p, 0, tall))
-        else:
-            keep(p, ratio * pull(p, 0, half) + pull(p, half, half))
-
+
+    part_copies = {}
+    for r in reversed(order):
+        if r:
+            back = nz - r
+            part_copies[back] = push(
+                part.at[pos[r]], part_in.at[back], part_sem, back, z_dev(r)
+            )
     own_score = own["score"]
     norms = {}
 
@@ -378,13 +398,6 @@
         weigh_again(p, 0, 4)
     for p in later:
         settle(p)
-    part_copies = {}
-    for r in reversed(order):
-        if r:
-            back = nz - r
-            part_copies[back] = push(
-                part.at[pos[r]], part_in.at[back], part_sem, back, z_dev(r)
-            )
     log_norm = norms[0]
     loss_ref[...] = log_norm - own_score
     own_term = jnp.exp(own_score - log_norm) - 1.0

time: 49.4 us -> 48.8 us (0.988)
  Pallas kernels: 48.7 us -> 48.1 us
    pallas_call x1, Pallas kernels: 47.8 us -> 47.2 us  [local(): pl.pallas_call(functools.partial(kernel, nz, nx), out_shape=(pltpu.VMEM((...]
where the time goes in v6:
time: 48.8 us; the launch traced here: 48.7 us
  Pallas kernels  48.1 us (99%)
  between operations  0.64 us (1%)
    pallas_call x1, Pallas kernels, local(): pl.pallas_call(functools.partial(kernel, nz, nx), out_shape=(pltpu.VMEM((...  47.2 us

profile of v6, /device:TPU:1, one launch (start us, length us, event | category | flops | bytes accessed | tf_op | source)
XLA Modules:
  0.0 48.7 jit_solution(12782368789446351596)
XLA Ops:
  0.6 47.2 %shard_map.93 = (f32[1,128]{1,0:T(1,128)S(1)}, f32[128,256]{1,0:T(8,128)S(1)}, f32[128,256]{1,0:T(8,128)S(1)}, bf16[512,256]{1,0:T(8,128)(2,1)S(1)}) custom-call(bf16[128,256]{1,0:T(8,128)(2,1)} %q_hbm.1, bf16[128,256]{1,0:T(8,128)(2,1)} %v_hbm.1, s32[4096]{0:T(1024)} %ids_hbm.1, bf16[512,256]{1,0:T(8,128)(2,1)} %neg_hbm.1, f32[4,128]{1,0:T(4,128)} %bitcast.4, ...), custom_call_target="tpu_custom_call" | custom-call | tf_op jit(solution)/shard_map/pallas_call | solution.py:519
  47.8 0.9 %shard_map.94 = (f32[1,128]{1,0:T(1,128)}, f32[128,256]{1,0:T(8,128)}, f32[128,256]{1,0:T(8,128)}, f32[512,256]{1,0:T(8,128)}) custom-call(f32[1,128]{1,0:T(1,128)S(1)} %get-tuple-element.12.loss_in, f32[128,256]{1,0:T(8,128)S(1)} %get-tuple-element.13.qg_in, f32[128,256]{1,0:T(8,128)S(1)} %get-tuple-element.14.vg_in, ...), custom_call_target="tpu_custom_call" | custom-call | tf_op jit(solution)/shard_map/pallas_call | solution.py:568

commit v7 on v6

--- a/solution.py
+++ b/solution.py
@@ -331,18 +331,22 @@
         totals[p] = weigh(p, 0, half, tops[p])
 
     first_round(split[0])
-    for copy in y_copies:
-        copy.wait_recv()
-    relay = push(
-        cand.at[rows_of(2 * shard, shard)],
-        cand.at[rows_of(3 * shard, shard)],
-        cand_sem,
-        3,
-        core_mate,
-    )
+    relays = []
+    for i, (lo, size) in enumerate(((0, cut_at), (cut_at, shard - cut_at))):
+        y_copies[i].wait_recv()
+        relays.append(
+            push(
+                cand.at[rows_of(2 * shard + lo, size)],
+                cand.at[rows_of(3 * shard + lo, size)],
+                cand_sem,
+                3 + i,
+                core_mate,
+            )
+        )
     for p in split[1:]:
         first_round(p)
-    relay.wait_recv()
+    for relay in relays:
+        relay.wait_recv()
     for p in split:
         top = jnp.maximum(tops[p], score(p, half, half))
         total = weigh(p, half, half, top)
@@ -552,7 +556,7 @@
             pltpu.VMEM((cut, width), bf16),
             dma((6,)),
             dma((2, nz + 1)),
-            dma((2, 4)),
+            dma((2, 5)),
             dma((2, 4)),
             dma((2, nz * pairs)),
             dma((2, nz)),

time: 48.8 us -> 48.9 us (level)
  no operation moved by 1% of the time
where the time goes in v7:
time: 48.9 us; the launch traced here: 48.8 us
  Pallas kernels  48.2 us (99%)
  between operations  0.64 us (1%)
    pallas_call x1, Pallas kernels, local(): pl.pallas_call(functools.partial(kernel, nz, nx), out_shape=(pltpu.VMEM((...  47.2 us

profile of v7, /device:TPU:1, one launch (start us, length us, event | category | flops | bytes accessed | tf_op | source)
XLA Modules:
  0.0 48.8 jit_solution(5332843823006295523)
XLA Ops:
  0.6 47.2 %shard_map.93 = (f32[1,128]{1,0:T(1,128)S(1)}, f32[128,256]{1,0:T(8,128)S(1)}, f32[128,256]{1,0:T(8,128)S(1)}, bf16[512,256]{1,0:T(8,128)(2,1)S(1)}) custom-call(bf16[128,256]{1,0:T(8,128)(2,1)} %q_hbm.1, bf16[128,256]{1,0:T(8,128)(2,1)} %v_hbm.1, s32[4096]{0:T(1024)} %ids_hbm.1, bf16[512,256]{1,0:T(8,128)(2,1)} %neg_hbm.1, f32[4,128]{1,0:T(4,128)} %bitcast.4, ...), custom_call_target="tpu_custom_call" | custom-call | tf_op jit(solution)/shard_map/pallas_call | solution.py:523
  47.9 0.9 %shard_map.94 = (f32[1,128]{1,0:T(1,128)}, f32[128,256]{1,0:T(8,128)}, f32[128,256]{1,0:T(8,128)}, f32[512,256]{1,0:T(8,128)}) custom-call(f32[1,128]{1,0:T(1,128)S(1)} %get-tuple-element.12.loss_in, f32[128,256]{1,0:T(8,128)S(1)} %get-tuple-element.13.qg_in, f32[128,256]{1,0:T(8,128)S(1)} %get-tuple-element.14.vg_in, ...), custom_call_target="tpu_custom_call" | custom-call | tf_op jit(solution)/shard_map/pallas_call | solution.py:572
